TPU v7x, 8 devices: a whole 2x2x1 slice. The times are simulated.
8 devices in a mesh: dp: 1 (over z), tp: 2 (over y), pp: 4 (over x, core).
Axes of the slice: x: 2, y: 2, z: 1, core: 2. Of those that a mesh axis runs over, the one named last changes fastest.
Arguments:
- x_in: bfloat16 [16, 4, 256, 1024], P('dp')
- g_out: float32 [16, 4, 256, 1024], P('dp')
- ln1_gain: float32 [4, 1024], P('pp')
- ln1_bias: float32 [4, 1024], P('pp')
- w_qkv: bfloat16 [4, 1024, 16, 3, 64], P('pp', None, 'tp')
- b_qkv: bfloat16 [4, 16, 3, 64], P('pp', 'tp')
- w_out: bfloat16 [4, 16, 64, 1024], P('pp', 'tp')
- b_out: bfloat16 [4, 1024], P('pp')
- ln2_gain: float32 [4, 1024], P('pp')
- ln2_bias: float32 [4, 1024], P('pp')
- w_up: bfloat16 [4, 1024, 4096], P('pp', None, 'tp')
- b_up: bfloat16 [4, 4096], P('pp', 'tp')
- w_down: bfloat16 [4, 4096, 1024], P('pp', 'tp')
- b_down: bfloat16 [4, 1024], P('pp')
Outputs:
- output 1: bfloat16 [16, 4, 256, 1024], P('dp')
- output 2: float32 [4, 1024], P(('dp', 'pp'))
- output 3: float32 [4, 1024], P(('dp', 'pp'))
- output 4: float32 [4, 1024, 16, 3, 64], P(('dp', 'pp'), None, 'tp')
- output 5: float32 [4, 16, 3, 64], P(('dp', 'pp'), 'tp')
- output 6: float32 [4, 16, 64, 1024], P(('dp', 'pp'), 'tp')
- output 7: float32 [4, 1024], P(('dp', 'pp'))
- output 8: float32 [4, 1024], P(('dp', 'pp'))
- output 9: float32 [4, 1024], P(('dp', 'pp'))
- output 10: float32 [4, 1024, 4096], P(('dp', 'pp'), None, 'tp')
- output 11: float32 [4, 4096], P(('dp', 'pp'), 'tp')
- output 12: float32 [4, 4096, 1024], P(('dp', 'pp'), 'tp')
- output 13: float32 [4, 1024], P(('dp', 'pp'))
All inputs are finite; a program needn't handle non-finite values.
Results may differ from a plain program's by a relative error of at most 0.0177431.
Values are sent between devices in bfloat16 or wider.
A program may use at most 1 GiB of HBM per device.

v0:
```python
import jax
import jax.numpy as jnp
from jax import lax
from jax.experimental import pallas as pl
from jax.experimental.pallas import tpu as pltpu
from jax.sharding import PartitionSpec as P

ROPE_BASE = 10000.0
LN_EPS = 1e-5
HEAD_DIM = 64
STAGE_SPECS = (P('pp', None), P('pp', None), P('pp', None, 'tp', None, None), P('pp', 'tp', None, None), P('pp', 'tp', None, None), P('pp', None), P('pp', None), P('pp', None), P('pp', None, 'tp'), P('pp', 'tp'), P('pp', 'tp', None), P('pp', None))
GRAD_SPECS = (P(('dp', 'pp'), None), P(('dp', 'pp'), None), P(('dp', 'pp'), None, 'tp', None, None), P(('dp', 'pp'), 'tp', None, None), P(('dp', 'pp'), 'tp', None, None), P(('dp', 'pp'), None), P(('dp', 'pp'), None), P(('dp', 'pp'), None), P(('dp', 'pp'), None, 'tp'), P(('dp', 'pp'), 'tp'), P(('dp', 'pp'), 'tp', None), P(('dp', 'pp'), None))
F32 = jnp.float32
BF16 = jnp.bfloat16
NN = (((1,), (0,)), ((), ()))
NT = (((1,), (1,)), ((), ()))
TN = (((0,), (0,)), ((), ()))


def dot(lhs, rhs, dims):
    return lax.dot_general(lhs, rhs, dims, preferred_element_type=F32)


def rotary_lanes(seq_len):
    rot_dim = HEAD_DIM // 4
    half_rot = rot_dim // 2
    inv_freq = ROPE_BASE ** (-(jnp.arange(half_rot, dtype=F32) * 2.0) / rot_dim)
    angles = jnp.arange(seq_len, dtype=F32)[:, None] * inv_freq[None, :]
    cos, sin = jnp.cos(angles), jnp.sin(angles)
    rest = HEAD_DIM - rot_dim
    zero_half, zero_rest = jnp.zeros_like(sin), jnp.zeros((seq_len, rest), F32)
    own = jnp.concatenate([cos, cos, jnp.ones((seq_len, rest), F32)], axis=1)
    above = jnp.concatenate([-sin, zero_half, zero_rest], axis=1)
    below = jnp.concatenate([zero_half, sin, zero_rest], axis=1)
    return jnp.stack([jnp.tile(tab, (1, 2)) for tab in (own, above, below)])


def rotate(values, tabs):
    return values * tabs[0] + pltpu.roll(values, 120, 1) * tabs[1] + pltpu.roll(values, 8, 1) * tabs[2]


def rotate_back(values, tabs):
    return values * tabs[0] + pltpu.roll(values * tabs[1], 8, 1) + pltpu.roll(values * tabs[2], 120, 1)


def pair_columns(pair, half_cols):
    pairs_per_half = half_cols // 3 // 128
    base = (pair // pairs_per_half) * half_cols + (pair % pairs_per_half) * 128
    return [pl.ds(pl.multiple_of(base + part * (half_cols // 3), 128), 128) for part in range(3)]


def softmax_rows(query, key, causal):
    scores = dot(query, key, NT) * (HEAD_DIM ** -0.5)
    scores = jnp.where(causal, scores, -1e30)
    expo = jnp.exp(scores - jnp.max(scores, axis=1, keepdims=True))
    return expo / jnp.sum(expo, axis=1, keepdims=True)


def attention_forward_kernel(tabs_ref, qkv_ref, ctx_ref):
    seq_len = qkv_ref.shape[0]
    half_cols = qkv_ref.shape[1] // 2
    causal = lax.broadcasted_iota(jnp.int32, (seq_len, seq_len), 0) >= lax.broadcasted_iota(jnp.int32, (seq_len, seq_len), 1)
    first = lax.broadcasted_iota(jnp.int32, (seq_len, 128), 1) < HEAD_DIM
    tabs = (tabs_ref[0], tabs_ref[1], tabs_ref[2])

    @pl.loop(0, ctx_ref.shape[1] // 128, unroll=2)
    def pair_step(pair):
        q_col, k_col, v_col = pair_columns(pair, half_cols)
        query = rotate(qkv_ref[:, q_col].astype(F32), tabs)
        key = rotate(qkv_ref[:, k_col].astype(F32), tabs).astype(BF16)
        value = qkv_ref[:, v_col]
        outs = []
        for keep in (first, ~first):
            probs = softmax_rows(jnp.where(keep, query, 0.0).astype(BF16), key, causal).astype(BF16)
            outs.append(dot(probs, value, NN))
        ctx_ref[:, pl.ds(pl.multiple_of(pair * 128, 128), 128)] = jnp.where(first, outs[0], outs[1]).astype(BF16)


def attention_backward_kernel(tabs_ref, qkv_ref, gctx_ref, gqkv_ref):
    seq_len = qkv_ref.shape[0]
    half_cols = qkv_ref.shape[1] // 2
    causal = lax.broadcasted_iota(jnp.int32, (seq_len, seq_len), 0) >= lax.broadcasted_iota(jnp.int32, (seq_len, seq_len), 1)
    first = lax.broadcasted_iota(jnp.int32, (seq_len, 128), 1) < HEAD_DIM
    tabs = (tabs_ref[0], tabs_ref[1], tabs_ref[2])

    @pl.loop(0, gctx_ref.shape[1] // 128)
    def pair_step(pair):
        q_col, k_col, v_col = pair_columns(pair, half_cols)
        query32 = rotate(qkv_ref[:, q_col].astype(F32), tabs)
        query = query32.astype(BF16)
        key = rotate(qkv_ref[:, k_col].astype(F32), tabs).astype(BF16)
        value = qkv_ref[:, v_col]
        gctx = gctx_ref[:, pl.ds(pl.multiple_of(pair * 128, 128), 128)]
        gctx32 = gctx.astype(F32)
        parts = []
        for keep in (first, ~first):
            probs = softmax_rows(jnp.where(keep, query32, 0.0).astype(BF16), key, causal)
            gprobs = dot(jnp.where(keep, gctx32, 0.0).astype(BF16), value, NT)
            gvalue = dot(probs.astype(BF16), gctx, TN)
            gscores = probs * (gprobs - jnp.sum(gprobs * probs, axis=1, keepdims=True))
            gscores = (gscores * (HEAD_DIM ** -0.5)).astype(BF16)
            parts.append((dot(gscores, key, NN), dot(gscores, query, TN), gvalue))
        gquery, gkey, gvalue = (jnp.where(first, one, two) for one, two in zip(*parts))
        gqkv_ref[:, q_col] = rotate_back(gquery, tabs).astype(BF16)
        gqkv_ref[:, k_col] = rotate_back(gkey, tabs).astype(BF16)
        gqkv_ref[:, v_col] = gvalue.astype(BF16)


def attention_call(kernel, tabs, seq_len, out_cols, n_dots, *arrays):
    tokens = arrays[0].shape[0]
    rows = tokens // seq_len
    width = arrays[0].shape[1] // 3
    heads = width // HEAD_DIM
    return pl.pallas_call(
        kernel,
        grid=(rows,),
        in_specs=[pl.BlockSpec(tabs.shape, lambda i: (0, 0, 0))] + [pl.BlockSpec((seq_len, array.shape[1]), lambda i: (i, 0)) for array in arrays],
        out_specs=pl.BlockSpec((seq_len, out_cols), lambda i: (i, 0)),
        out_shape=jax.ShapeDtypeStruct((tokens, out_cols), BF16),
        compiler_params=pltpu.CompilerParams(dimension_semantics=('arbitrary',), vmem_limit_bytes=48 * 1024 * 1024),
        cost_estimate=pl.CostEstimate(flops=2 * n_dots * rows * heads * seq_len * seq_len * 256, bytes_accessed=2 * tokens * (sum(a.shape[1] for a in arrays) + out_cols), transcendentals=rows * heads * seq_len * seq_len),
    )(tabs, *arrays)


def normalize(hidden):
    hidden_f = hidden.astype(F32)
    center = hidden_f - jnp.mean(hidden_f, axis=-1, keepdims=True)
    inv_std = lax.rsqrt(jnp.mean(center * center, axis=-1, keepdims=True) + LN_EPS)
    return center * inv_std, inv_std


def gelu_parts(pre_act):
    cdf = 0.5 * (1.0 + lax.erf(pre_act * (2.0 ** -0.5)))
    return cdf


def solution(mesh):
    everyone = ('pp', 'tp')

    def device_fn(x_in, g_out, ln1_gain, ln1_bias, w_qkv, b_qkv, w_out, b_out, ln2_gain, ln2_bias, w_up, b_up, w_down, b_down):
        n_stages, tp_size = mesh.shape['pp'], mesh.shape['tp']
        n_dev = n_stages * tp_size
        stage_id = lax.axis_index('pp')
        rank = stage_id * tp_size + lax.axis_index('tp')
        n_micro, n_rows, seq_len, width = x_in.shape
        own_micro = n_micro // n_dev
        tokens = own_micro * n_rows * seq_len
        tabs = rotary_lanes(seq_len)

        def gather(shard):
            return lax.all_gather(shard, everyone, axis=0, tiled=True)

        heads = w_qkv.shape[2]
        qkv_shard = jnp.transpose(w_qkv[0], (2, 1, 3, 0)).reshape(3 * heads * HEAD_DIM, width)
        up_shard = jnp.transpose(w_up[0])
        out_shard = w_out[0].reshape(heads * HEAD_DIM, width)
        all_qkv = gather(qkv_shard)
        all_out = gather(out_shard)
        all_up = gather(up_shard)
        all_down = gather(w_down[0])

        def small(own, columns):
            return own.reshape(1, columns).astype(F32)

        b_qkv_own = jnp.transpose(b_qkv[0], (1, 0, 2)).reshape(1, -1)
        vec_own = jnp.concatenate([small(b_qkv_own, 3 * heads * HEAD_DIM), small(b_up, b_up.shape[1]), ln1_gain, ln1_bias, ln2_gain, ln2_bias, small(b_out, width), small(b_down, width)], axis=1)
        vec_all = gather(vec_own).reshape(n_stages, tp_size, -1)
        cut = 0

        def take(columns, split):
            nonlocal cut
            part = vec_all[:, :, cut:cut + columns] if split else vec_all[:, 0, cut:cut + columns]
            cut += columns
            return part.reshape(n_stages, -1)

        bias_qkv = take(3 * heads * HEAD_DIM, True)
        bias_up = take(b_up.shape[1], True)
        gain1, shift1, gain2, shift2, bias_out, bias_down = (take(width, False) for _ in range(6))

        def layer(stack, index):
            rows = stack.shape[0] // n_stages
            return stack[index * rows:(index + 1) * rows]

        x_own = lax.dynamic_slice_in_dim(x_in, rank * own_micro, own_micro, 0).reshape(tokens, width)
        g_own = lax.dynamic_slice_in_dim(g_out, rank * own_micro, own_micro, 0).reshape(tokens, width).astype(BF16)

        hidden = x_own
        saved = []
        for index in range(n_stages):
            normed, _ = normalize(hidden)
            normed_a = (normed * gain1[index] + shift1[index]).astype(BF16)
            normed_m = (normed * gain2[index] + shift2[index]).astype(BF16)
            qkv_proj = (dot(normed_a, layer(all_qkv, index), NT) + bias_qkv[index]).astype(BF16)
            context = attention_call(attention_forward_kernel, tabs, seq_len, width, 2, qkv_proj)
            pre_act = dot(normed_m, layer(all_up, index), NT) + bias_up[index]
            hidden_mlp = (pre_act * gelu_parts(pre_act)).astype(BF16)
            attn_sum = dot(context, layer(all_out, index), NN)
            mlp_sum = dot(hidden_mlp, layer(all_down, index), NN)
            saved.append((hidden, normed_a, normed_m, qkv_proj, context, pre_act, hidden_mlp))
            hidden = (hidden.astype(F32) + attn_sum + bias_out[index] + mlp_sum + bias_down[index]).astype(BF16)
        y_out = gather(hidden).reshape(x_in.shape)

        grad = g_own
        wgrads = {name: [None] * n_stages for name in ('qkv', 'out', 'up', 'down')}
        vgrads = [None] * n_stages
        for index in reversed(range(n_stages)):
            hidden, normed_a, normed_m, qkv_proj, context, pre_act, hidden_mlp = saved[index]
            grad_f = grad.astype(F32)
            wgrads['down'][index] = dot(hidden_mlp, grad, TN).astype(BF16)
            grad_mlp = dot(grad, layer(all_down, index), NT)
            slope = gelu_parts(pre_act) + pre_act * jnp.exp(-0.5 * pre_act * pre_act) * ((2.0 * jnp.pi) ** -0.5)
            grad_pre = grad_mlp * slope
            grad_pre_b = grad_pre.astype(BF16)
            wgrads['up'][index] = dot(grad_pre_b, normed_m, TN).astype(BF16)
            wgrads['out'][index] = dot(context, grad, TN).astype(BF16)
            grad_context = dot(grad, layer(all_out, index), NT).astype(BF16)
            grad_qkv = attention_call(attention_backward_kernel, tabs, seq_len, 3 * width, 5, qkv_proj, grad_context)
            wgrads['qkv'][index] = dot(grad_qkv, normed_a, TN).astype(BF16)
            grad_m = dot(grad_pre_b, layer(all_up, index), NN)
            grad_a = dot(grad_qkv, layer(all_qkv, index), NN)
            normed, inv_std = normalize(hidden)
            grad_n = grad_a * gain1[index] + grad_m * gain2[index]
            mean_g = jnp.mean(grad_n, axis=-1, keepdims=True)
            mean_gn = jnp.mean(grad_n * normed, axis=-1, keepdims=True)
            vgrads[index] = (jnp.sum(grad_qkv.astype(F32), axis=0), jnp.sum(grad_pre, axis=0), jnp.sum(grad_a * normed, axis=0), jnp.sum(grad_a, axis=0), jnp.sum(grad_m * normed, axis=0), jnp.sum(grad_m, axis=0), jnp.sum(grad_f, axis=0))
            grad = (grad_f + inv_std * (grad_n - mean_g - normed * mean_gn)).astype(BF16)

        def scatter(parts):
            return lax.psum_scatter(jnp.concatenate(parts, axis=0), everyone, scatter_dimension=0, tiled=True).astype(F32)

        own = {name: scatter(parts) for name, parts in wgrads.items()}
        vec = jnp.stack([jnp.concatenate(parts) for parts in vgrads])
        vec = lax.dynamic_index_in_dim(lax.psum(vec, everyone), stage_id, 0, keepdims=False)
        sizes = [3 * width, b_up.shape[1] * tp_size] + [width] * 5
        pieces, cut = [], 0
        for size in sizes:
            pieces.append(vec[cut:cut + size])
            cut += size
        tp_rank = lax.axis_index('tp')
        d_bqkv = lax.dynamic_index_in_dim(pieces[0].reshape(tp_size, 3, heads, HEAD_DIM), tp_rank, 0, keepdims=False)
        d_bup = lax.dynamic_index_in_dim(pieces[1].reshape(tp_size, -1), tp_rank, 0, keepdims=False)
        d_qkv = jnp.transpose(own['qkv'].reshape(3, heads, HEAD_DIM, width), (3, 1, 0, 2))
        grads = (pieces[2], pieces[3], d_qkv, jnp.transpose(d_bqkv, (1, 0, 2)), own['out'].reshape(heads, HEAD_DIM, width), pieces[6], pieces[4], pieces[5], jnp.transpose(own['up']), d_bup, own['down'], pieces[6])
        return tuple([y_out] + [value[None] for value in grads])

    return jax.shard_map(device_fn, mesh=mesh, in_specs=(P('dp'), P('dp')) + STAGE_SPECS, out_specs=(P('dp'),) + GRAD_SPECS, check_vma=False)
```

profile of v0, /device:TPU:0, one launch (start us, length us, event | category | flops | bytes accessed | tf_op | source)
XLA Modules:
  0.0 2526.0 jit_solution(1629880556472157179)
XLA Ops:
  72.2 112.3 %all-gather.8.cloned.1.call-done = bf16[12288,1024]{1,0:T(8,128)(2,1)} async-done(((bf16[1536,1024]{1,0:T(8,128)(2,1)}), bf16[12288,1024]{1,0:T(8,128)(2,1)}) %all-gather.8.cloned.1.call-update) | async-done | bytes 25165840 | tf_op jit(solution)/shard_map/all_gather | solution.py:151
  203.9 40.9 %shard_map.237 = bf16[2048,1024]{1,0:T(8,128)(2,1)S(1)} custom-call(f32[3,256,128]{2,1,0:T(8,128)S(1)} %pad_maximum_fusion.4.tabs_ref, bf16[2048,3072]{1,0:T(8,128)(2,1)} %add_convert_fusion.3.qkv_ref), custom_call_target="tpu_custom_call" | custom-call | flops 8589934592 | bytes 16777216 | tf_op jit(solution)/shard_map/pallas_call | solution.py:114
  256.2 85.3 %all-gather.12.cloned.1.call-done = bf16[16384,1024]{0,1:T(8,128)(2,1)} async-done(((bf16[2048,1024]{0,1:T(8,128)(2,1)}), bf16[16384,1024]{0,1:T(8,128)(2,1)}) %all-gather.12.cloned.1.call-update) | async-done | bytes 33554448 | tf_op jit(solution)/shard_map/all_gather | solution.py:151
  341.5 29.7 %multiply_convert_fusion.3 = (bf16[2048,4096]{1,0:T(8,128)(2,1)}, f32[2048,4096]{1,0:T(8,128)}) fusion(f32[4096]{0:T(1024)S(1)} %bitcast.254, bf16[2048,1024]{1,0:T(8,128)(2,1)} %get-tuple-element.85, bf16[16384,1024]{0,1:T(8,128)(2,1)} %all-gather.12.cloned.1.call-done), kind=kOutput, calls=%fused_computation.32 | convolution fusion | flops 17230200832 | bytes 62930944 | tf_op jit(solution)/shard_map/dot_general | solution.py:21
  371.2 127.1 %all-gather.16.cloned.1.call-done = bf16[1,16384,1024]{2,1,0:T(8,128)(2,1)} async-done(((bf16[1,2048,1024]{2,1,0:T(8,128)(2,1)}), bf16[1,16384,1024]{2,1,0:T(8,128)(2,1)}) %all-gather.16.cloned.1.call-update) | async-done | bytes 33554448 | tf_op jit(solution)/shard_map/all_gather | solution.py:151
  544.1 40.7 %shard_map.238 = bf16[2048,1024]{1,0:T(8,128)(2,1)S(1)} custom-call(f32[3,256,128]{2,1,0:T(8,128)S(1)} %pad_maximum_fusion.4.tabs_ref, bf16[2048,3072]{1,0:T(8,128)(2,1)} %add_convert_fusion.2.qkv_ref), custom_call_target="tpu_custom_call" | custom-call | flops 8589934592 | bytes 16777216 | tf_op jit(solution)/shard_map/pallas_call | solution.py:114
  670.8 40.7 %shard_map.239 = bf16[2048,1024]{1,0:T(8,128)(2,1)S(1)} custom-call(f32[3,256,128]{2,1,0:T(8,128)S(1)} %pad_maximum_fusion.4.tabs_ref, bf16[2048,3072]{1,0:T(8,128)(2,1)} %add_convert_fusion.1.qkv_ref), custom_call_target="tpu_custom_call" | custom-call | flops 8589934592 | bytes 16777216 | tf_op jit(solution)/shard_map/pallas_call | solution.py:114
  795.6 40.8 %shard_map.240 = bf16[2048,1024]{1,0:T(8,128)(2,1)S(1)} custom-call(f32[3,256,128]{2,1,0:T(8,128)S(1)} %pad_maximum_fusion.4.tabs_ref, bf16[2048,3072]{1,0:T(8,128)(2,1)} %add_convert_fusion.qkv_ref), custom_call_target="tpu_custom_call" | custom-call | flops 8589934592 | bytes 16777216 | tf_op jit(solution)/shard_map/pallas_call | solution.py:114
  838.4 93.6 %shard_map.241 = bf16[2048,3072]{1,0:T(8,128)(2,1)} custom-call(f32[3,256,128]{2,1,0:T(8,128)S(1)} %pad_maximum_fusion.4.tabs_ref, bf16[2048,3072]{1,0:T(8,128)(2,1)} %add_convert_fusion.qkv_ref, bf16[2048,1024]{1,0:T(8,128)(2,1)S(1)} %copy-done.8), custom_call_target="tpu_custom_call" | custom-call | flops 21474836480 | bytes 29360128 | tf_op jit(solution)/shard_map/pallas_call | solution.py:114
  986.7 37.9 %fusion.207 = (f32[4096]{0:T(1024)}, bf16[2048,4096]{1,0:T(8,128)(2,1)}) fusion(f32[2048,4096]{1,0:T(8,128)} %get-tuple-element.156, f32[4096]{0:T(1024)S(1)} %bitcast.261, bf16[2048,1024]{1,0:T(8,128)(2,1)} %bitcast.226, bf16[1,16384,1024]{2,1,0:T(8,128)(2,1)} %all-gather.16.cloned.1.call-done), kind=kOutput, calls=%fused_computation.321 | convolution fusion | flops 17280528384 | bytes 62947328 | tf_op jit(solution)/shard_map/dot_general | solution.py:21
  1024.6 28.9 %fusion.197 = (f32[2048]{0:T(1024)S(1)}, f32[2048]{0:T(1024)S(1)}, f32[2048,1024]{1,0:T(8,128)}, f32[1024]{0:T(1024)}, f32[1024]{0:T(1024)}, /*index=5*/f32[1024]{0:T(1024)}, f32[1024]{0:T(1024)}) fusion(f32[2048]{0:T(1024)S(1)} %add_rsqrt_fusion, f32[2048]{0:T(1024)S(1)} %broadcast_multiply_fusion.6, bf16[2048,1024]{1,0:T(8,128)(2,1)S(1)} %copy-done.10, ...), kind=kOutput, calls=%fused_computation.314 | convolution fusion | flops 17211322368 | bytes 46194688 | tf_op jit(solution)/shard_map/dot_general | solution.py:21
  1073.2 93.9 %shard_map.242 = bf16[2048,3072]{1,0:T(8,128)(2,1)} custom-call(f32[3,256,128]{2,1,0:T(8,128)S(1)} %pad_maximum_fusion.4.tabs_ref, bf16[2048,3072]{1,0:T(8,128)(2,1)} %add_convert_fusion.1.qkv_ref, bf16[2048,1024]{1,0:T(8,128)(2,1)S(1)} %convolution_convert_fusion.10.gctx_ref), custom_call_target="tpu_custom_call" | custom-call | flops 21474836480 | bytes 29360128 | tf_op jit(solution)/shard_map/pallas_call | solution.py:114
  1193.6 37.3 %fusion.208 = (f32[4096]{0:T(1024)}, bf16[2048,4096]{1,0:T(8,128)(2,1)}) fusion(f32[2048,4096]{1,0:T(8,128)} %get-tuple-element.152, f32[4096]{0:T(1024)S(1)} %bitcast.259, bf16[2048,1024]{1,0:T(8,128)(2,1)S(1)} %copy-done.26, bf16[1,16384,1024]{2,1,0:T(8,128)(2,1)} %all-gather.16.cloned.1.call-done), kind=kOutput, calls=%fused_computation.322 | convolution fusion | flops 17280528384 | bytes 62947328 | tf_op jit(solution)/shard_map/dot_general | solution.py:21
  1230.9 28.9 %fusion.194 = (f32[2048]{0:T(1024)S(1)}, f32[2048]{0:T(1024)S(1)}, f32[2048,1024]{1,0:T(8,128)}, f32[1024]{0:T(1024)}, f32[1024]{0:T(1024)}, /*index=5*/f32[1024]{0:T(1024)}, f32[1024]{0:T(1024)}) fusion(f32[2048]{0:T(1024)S(1)} %copy-done.52, f32[2048]{0:T(1024)S(1)} %copy-done.37, bf16[2048,1024]{1,0:T(8,128)(2,1)S(1)} %copy-done.20, ...), kind=kOutput, calls=%fused_computation.311 | convolution fusion | flops 17211322368 | bytes 46194688 | tf_op jit(solution)/shard_map/dot_general | solution.py:21
  1279.6 93.8 %shard_map.243 = bf16[2048,3072]{1,0:T(8,128)(2,1)} custom-call(f32[3,256,128]{2,1,0:T(8,128)S(1)} %pad_maximum_fusion.4.tabs_ref, bf16[2048,3072]{1,0:T(8,128)(2,1)} %add_convert_fusion.2.qkv_ref, bf16[2048,1024]{1,0:T(8,128)(2,1)S(1)} %convolution_convert_fusion.9.gctx_ref), custom_call_target="tpu_custom_call" | custom-call | flops 21474836480 | bytes 29360128 | tf_op jit(solution)/shard_map/pallas_call | solution.py:114
  1399.8 37.3 %fusion.209 = (f32[4096]{0:T(1024)}, bf16[2048,4096]{1,0:T(8,128)(2,1)}) fusion(f32[2048,4096]{1,0:T(8,128)} %get-tuple-element.148, f32[4096]{0:T(1024)S(1)} %bitcast.257, bf16[2048,1024]{1,0:T(8,128)(2,1)S(1)} %copy-done.28, bf16[1,16384,1024]{2,1,0:T(8,128)(2,1)} %all-gather.16.cloned.1.call-done), kind=kOutput, calls=%fused_computation.323 | convolution fusion | flops 17280528384 | bytes 62947328 | tf_op jit(solution)/shard_map/dot_general | solution.py:21
  1437.1 29.1 %fusion.191 = (f32[2048]{0:T(1024)S(1)}, f32[2048]{0:T(1024)S(1)}, f32[2048,1024]{1,0:T(8,128)}, f32[1024]{0:T(1024)}, f32[1024]{0:T(1024)}, /*index=5*/f32[1024]{0:T(1024)}, f32[1024]{0:T(1024)}) fusion(f32[2048]{0:T(1024)S(1)} %copy-done.49, f32[2048]{0:T(1024)S(1)} %copy-done.34, bf16[2048,1024]{1,0:T(8,128)(2,1)S(1)} %copy-done.15, ...), kind=kOutput, calls=%fused_computation.308 | convolution fusion | flops 17211322368 | bytes 46194688 | tf_op jit(solution)/shard_map/dot_general | solution.py:21
  1491.7 93.7 %shard_map.244 = bf16[2048,3072]{1,0:T(8,128)(2,1)} custom-call(f32[3,256,128]{2,1,0:T(8,128)S(1)} %pad_maximum_fusion.4.tabs_ref, bf16[2048,3072]{1,0:T(8,128)(2,1)} %add_convert_fusion.3.qkv_ref, bf16[2048,1024]{1,0:T(8,128)(2,1)S(1)} %convolution_convert_fusion.8.gctx_ref), custom_call_target="tpu_custom_call" | custom-call | flops 21474836480 | bytes 29360128 | tf_op jit(solution)/shard_map/pallas_call | solution.py:114
  1592.2 37.6 %fusion.210 = (f32[4096]{0:T(1024)S(1)}, bf16[2048,4096]{1,0:T(8,128)(2,1)}) fusion(f32[2048,4096]{1,0:T(8,128)} %get-tuple-element.144, f32[4096]{0:T(1024)S(1)} %bitcast.255, bf16[2048,1024]{1,0:T(8,128)(2,1)} %copy-done.30, bf16[1,16384,1024]{2,1,0:T(8,128)(2,1)} %all-gather.16.cloned.1.call-done), kind=kOutput, calls=%fused_computation.324 | convolution fusion | flops 17280528384 | bytes 62947328 | tf_op jit(solution)/shard_map/dot_general | solution.py:21
  1888.4 35.9 %pad_maximum_fusion = bf16[16384,1024]{1,0:T(8,128)(2,1)} fusion(bf16[4096,1024]{1,0:T(8,128)(2,1)} %fusion.123, bf16[4096,1024]{1,0:T(8,128)(2,1)} %fusion.126, bf16[4096,1024]{1,0:T(8,128)(2,1)} %fusion.129, bf16[4096,1024]{1,0:T(8,128)(2,1)} %fusion.132), kind=kLoop, calls=%fused_computation.24 | loop fusion | flops 134217728 | bytes 67108864 | tf_op jit(solution)/shard_map/concatenate | solution.py:229
  2017.5 36.3 %pad_maximum_fusion.1 = bf16[16384,1024]{1,0:T(8,128)(2,1)} fusion(bf16[4096,1024]{1,0:T(8,128)(2,1)} %convolution_convert_fusion, bf16[4096,1024]{1,0:T(8,128)(2,1)} %convolution_convert_fusion.1, bf16[4096,1024]{1,0:T(8,128)(2,1)} %convolution_convert_fusion.2, bf16[4096,1024]{1,0:T(8,128)(2,1)} %convolution_convert_fusion.3), kind=kLoop, calls=%fused_computation.25 | loop fusion | flops 134217728 | bytes 67108864 | tf_op jit(solution)/shard_map/concatenate | solution.py:229
  2103.5 34.1 %reduce-scatter.9.cloned.1.call-done = bf16[2048,1024]{1,0:T(8,128)(2,1)} async-done(((bf16[16384,1024]{1,0:T(8,128)(2,1)}), bf16[2048,1024]{1,0:T(8,128)(2,1)}) %reduce-scatter.9.cloned.1.call-update) | async-done | bytes 4194320 | tf_op jit(solution)/shard_map/reduce_scatter | solution.py:229
  2154.1 184.2 %reduce-scatter.11.cloned.1.call-done = bf16[2048,1024]{1,0:T(8,128)(2,1)} async-done(((bf16[16384,1024]{1,0:T(8,128)(2,1)}), bf16[2048,1024]{1,0:T(8,128)(2,1)}) %reduce-scatter.11.cloned.1.call-update) | async-done | bytes 4194320 | tf_op jit(solution)/shard_map/reduce_scatter | solution.py:229
  2345.8 149.3 %all-gather.14.cloned.1.call-done = bf16[16384,1024]{1,0:T(8,128)(2,1)} async-done(((bf16[2048,1024]{1,0:T(8,128)(2,1)}), bf16[16384,1024]{1,0:T(8,128)(2,1)}) %all-gather.14.cloned.1.call-update) | async-done | bytes 33554448 | tf_op jit(solution)/shard_map/all_gather | solution.py:151
  (462 shorter events, 940.0 us)
Async XLA Ops:
  7.2 55.3 %all-gather.10.cloned.1.call-start = ((), (), s32[]{:S(2)}) async-start(), calls=%async_computation.5 | async-start | bytes 9437184 | tf_op jit(solution)/shard_map/all_gather | solution.py:151
  7.9 176.6 %all-gather.8.cloned.1.call-start = ((), (), s32[]{:S(2)}) async-start(), calls=%async_computation.4 | async-start | bytes 28311552 | tf_op jit(solution)/shard_map/all_gather | solution.py:151
  12.0 329.5 %all-gather.12.cloned.1.call-start = ((), (), s32[]{:S(2)}) async-start(), calls=%async_computation.6 | async-start | bytes 37748736 | tf_op jit(solution)/shard_map/all_gather | solution.py:151
  12.7 485.6 %all-gather.16.cloned.1.call-start = ((), (), s32[]{:S(2)}) async-start(), calls=%async_computation.13 | async-start | bytes 37748736 | tf_op jit(solution)/shard_map/all_gather | solution.py:151
  13.3 2077.1 %all-reduce.2.cloned.1.call-start = ((), (), s32[]{:S(2)}) async-start(), calls=%async_computation.8 | async-start | bytes 393216 | tf_op jit(solution)/shard_map/psum | solution.py:233
  37.4 304.1 %copy-start.57 = (f32[1,16,2,128]{3,1,2,0:T(8,128)}, f32[1,16,2,128]{3,1,2,0:T(8,128)S(1)}, u32[]{:S(2)}) copy-start(f32[1,16,2,128]{3,1,2,0:T(8,128)S(1)} %copy.44) | copy-start | bytes 49156
  523.1 99.6 %copy-start.14 = (bf16[2048,1024]{1,0:T(8,128)(2,1)}, bf16[2048,1024]{1,0:T(8,128)(2,1)S(1)}, u32[]{:S(2)}) copy-start(bf16[2048,1024]{1,0:T(8,128)(2,1)S(1)} %get-tuple-element.146) | copy-start | bytes 12582916
  523.1 71.5 %copy-start.33 = (f32[2048]{0:T(1024)}, f32[2048]{0:T(1024)S(1)}, u32[]{:S(2)}) copy-start(f32[2048]{0:T(1024)S(1)} %broadcast_multiply_fusion.8) | copy-start | bytes 24580
  524.5 70.1 %copy-start.48 = (f32[2048]{0:T(1024)}, f32[2048]{0:T(1024)S(1)}, u32[]{:S(2)}) copy-start(f32[2048]{0:T(1024)S(1)} %add_rsqrt_fusion.2) | copy-start | bytes 24580
  646.9 74.8 %copy-start.36 = (f32[2048]{0:T(1024)}, f32[2048]{0:T(1024)S(1)}, u32[]{:S(2)}) copy-start(f32[2048]{0:T(1024)S(1)} %broadcast_multiply_fusion.7) | copy-start | bytes 24580
  650.3 71.4 %copy-start.51 = (f32[2048]{0:T(1024)}, f32[2048]{0:T(1024)S(1)}, u32[]{:S(2)}) copy-start(f32[2048]{0:T(1024)S(1)} %add_rsqrt_fusion.1) | copy-start | bytes 24580
  774.6 278.8 %copy-start.39 = (f32[2048]{0:T(1024)}, f32[2048]{0:T(1024)S(1)}, u32[]{:S(2)}) copy-start(f32[2048]{0:T(1024)S(1)} %broadcast_multiply_fusion.6) | copy-start | bytes 24580
  776.1 277.4 %copy-start.54 = (f32[2048]{0:T(1024)}, f32[2048]{0:T(1024)S(1)}, u32[]{:S(2)}) copy-start(f32[2048]{0:T(1024)S(1)} %add_rsqrt_fusion) | copy-start | bytes 24580
  795.6 42.8 %copy-start.8 = (bf16[2048,1024]{1,0:T(8,128)(2,1)S(1)}, bf16[2048,1024]{1,0:T(8,128)(2,1)}, u32[]{:S(2)}) copy-start(bf16[2048,1024]{1,0:T(8,128)(2,1)} %convolution_convert_fusion.11.gctx_ref) | copy-start | bytes 12582916
  1585.5 44.4 %slice-start.3 = ((s8[12582912]{0:T(1024)(128)(4,1)}), s8[4194304]{0:T(1024)(128)(4,1)S(1)}, s32[]{:S(2)}) async-start(s8[12582912]{0:T(1024)(128)(4,1)} %bitcast.231), calls=%async_computation.17 | async-start | bytes 8388608
  1675.7 419.4 %reduce-scatter.7.cloned.1.call-start = ((), (), s32[]{:S(2)}) async-start(), calls=%async_computation.10 | async-start | bytes 9437184 | tf_op jit(solution)/shard_map/reduce_scatter | solution.py:229
  1682.3 415.7 %reduce-scatter.5.cloned.1.call-start = ((), (), s32[]{:S(2)}) async-start(), calls=%async_computation.9 | async-start | bytes 28311552 | tf_op jit(solution)/shard_map/reduce_scatter | solution.py:229
  1701.7 39.5 %slice-start = ((s8[12582912]{0:T(1024)(128)(4,1)}), s8[4194304]{0:T(1024)(128)(4,1)S(1)}, s32[]{:S(2)}) async-start(s8[12582912]{0:T(1024)(128)(4,1)} %bitcast.229), calls=%async_computation.14 | async-start | bytes 8388608
  1787.0 350.6 %reduce-scatter.9.cloned.1.call-start = ((), (), s32[]{:S(2)}) async-start(), calls=%async_computation.11 | async-start | bytes 37748736 | tf_op jit(solution)/shard_map/reduce_scatter | solution.py:229
  1924.4 413.9 %reduce-scatter.11.cloned.1.call-start = ((), (), s32[]{:S(2)}) async-start(), calls=%async_computation.12 | async-start | bytes 37748736 | tf_op jit(solution)/shard_map/reduce_scatter | solution.py:229
  1948.9 48.8 %slice-start.6 = ((s8[16777216]{0:T(1024)(128)(4,1)}), s8[4194304]{0:T(1024)(128)(4,1)S(1)}, s32[]{:S(2)}) async-start(s8[16777216]{0:T(1024)(128)(4,1)} %bitcast.300), calls=%async_computation.20 | async-start | bytes 8388608
  1948.9 48.8 %slice-start.7 = ((s8[16777216]{0:T(1024)(128)(4,1)}), s8[4194304]{0:T(1024)(128)(4,1)S(1)}, s32[]{:S(2)}) async-start(s8[16777216]{0:T(1024)(128)(4,1)} %bitcast.300), calls=%async_computation.21 | async-start | bytes 8388608
  2053.9 441.2 %all-gather.14.cloned.1.call-start = ((), (), s32[]{:S(2)}) async-start(), calls=%async_computation.7 | async-start | bytes 37748736 | tf_op jit(solution)/shard_map/all_gather | solution.py:151
  2093.8 401.3 %copy-start.67 = (f32[1,1024]{1,0:T(1,128)}, f32[1,1024]{1,0:T(1,128)S(1)}, u32[]{:S(2)}) copy-start(f32[1,1024]{1,0:T(1,128)S(1)} %get-tuple-element.219) | copy-start | bytes 12292
  (125 other events, 2639.5 us)
Sparse Core Ops, SparseCore 0:
  9.8 52.6 all-gather.9
  64.9 119.6 all-gather.7
  186.4 155.1 all-gather.11
  343.2 155.0 all-gather.15
  1675.8 42.6 all-reduce.1
  1722.3 62.5 reduce-scatter.6
  1788.4 147.9 reduce-scatter.4
  1940.5 197.1 reduce-scatter.8
  2141.1 197.1 reduce-scatter.10
  2340.0 155.0 all-gather.13
where the time goes:
time: 2530 us
  matrix products  993 us (39%)
  waiting for transfers between devices  697 us (28%)
  Pallas kernels  538 us (21%)
  other arithmetic  206 us (8%)
  local copies, waits for them, and re-layouts  59.2 us (2%)
    dot_general x48, matrix products, dot(): return lax.dot_general(lhs, rhs, dims, preferred_element_type=F32)  993 us
    pallas_call x8, Pallas kernels, attention_call(): pl.pallas_call(kernel, grid=(rows,), in_specs=[pl.BlockSpec(tabs.shape, l...  538 us
    all_gather x5, waiting for transfers between devices, gather(): return lax.all_gather(shard, everyone, axis=0, tiled=True)  477 us
    reduce_scatter x4, waiting for transfers between devices, scatter(): lax.psum_scatter(jnp.concatenate(parts, axis=0), everyone, scatter_dimens...  218 us
    concatenate x4, other arithmetic, scatter(): jnp.concatenate(parts, axis=0)  107 us
  transfers between devices with their start and end apart: 10, of which 7 were waited for; matrix products, arithmetic and copies ran while one was open for 22% of the time, Pallas kernels for 2%

commit v1 on v0

v1 whole, which is shorter than its diff:
```python
import jax
import jax.numpy as jnp
from jax import lax
from jax.experimental import pallas as pl
from jax.experimental.layout import Layout, with_layout_constraint
from jax.experimental.pallas import tpu as pltpu
from jax.sharding import PartitionSpec as P

ROPE_BASE = 10000.0
LN_EPS = 1e-5
HEAD_DIM = 64
STAGE_SPECS = (P('pp', None), P('pp', None), P('pp', None, 'tp', None, None), P('pp', 'tp', None, None), P('pp', 'tp', None, None), P('pp', None), P('pp', None), P('pp', None), P('pp', None, 'tp'), P('pp', 'tp'), P('pp', 'tp', None), P('pp', None))
GRAD_SPECS = (P(('dp', 'pp'), None), P(('dp', 'pp'), None), P(('dp', 'pp'), None, 'tp', None, None), P(('dp', 'pp'), 'tp', None, None), P(('dp', 'pp'), 'tp', None, None), P(('dp', 'pp'), None), P(('dp', 'pp'), None), P(('dp', 'pp'), None), P(('dp', 'pp'), None, 'tp'), P(('dp', 'pp'), 'tp'), P(('dp', 'pp'), 'tp', None), P(('dp', 'pp'), None))
F32 = jnp.float32
BF16 = jnp.bfloat16
NN = (((1,), (0,)), ((), ()))
NT = (((1,), (1,)), ((), ()))
TN = (((0,), (0,)), ((), ()))


def dot(lhs, rhs, dims):
    return lax.dot_general(lhs, rhs, dims, preferred_element_type=F32)


def rotary_lanes(seq_len):
    rot_dim = HEAD_DIM // 4
    half_rot = rot_dim // 2
    inv_freq = ROPE_BASE ** (-(jnp.arange(half_rot, dtype=F32) * 2.0) / rot_dim)
    angles = jnp.arange(seq_len, dtype=F32)[:, None] * inv_freq[None, :]
    cos, sin = jnp.cos(angles), jnp.sin(angles)
    rest = HEAD_DIM - rot_dim
    zero_half, zero_rest = jnp.zeros_like(sin), jnp.zeros((seq_len, rest), F32)
    own = jnp.concatenate([cos, cos, jnp.ones((seq_len, rest), F32)], axis=1)
    above = jnp.concatenate([-sin, zero_half, zero_rest], axis=1)
    below = jnp.concatenate([zero_half, sin, zero_rest], axis=1)
    return jnp.stack([jnp.tile(tab, (1, 2)) for tab in (own, above, below)])


def rotate(values, tabs):
    return values * tabs[0] + pltpu.roll(values, 120, 1) * tabs[1] + pltpu.roll(values, 8, 1) * tabs[2]


def rotate_back(values, tabs):
    return values * tabs[0] + pltpu.roll(values * tabs[1], 8, 1) + pltpu.roll(values * tabs[2], 120, 1)


def pair_columns(pair, half_cols):
    pairs_per_half = half_cols // 3 // 128
    base = (pair // pairs_per_half) * half_cols + (pair % pairs_per_half) * 128
    return [pl.ds(pl.multiple_of(base + part * (half_cols // 3), 128), 128) for part in range(3)]


def transposed_probs(key, query, causal):
    half = key.shape[0] // 2
    top = dot(key[:half], query, NT)
    low = dot(key[half:], query[half:], NT)
    left = jnp.where(causal, top[:, :half], -1e30)
    right = top[:, half:]
    low = jnp.where(causal, low, -1e30)
    max_left = jnp.max(left, axis=0, keepdims=True)
    max_right = jnp.maximum(jnp.max(right, axis=0, keepdims=True), jnp.max(low, axis=0, keepdims=True))
    left, right, low = jnp.exp(left - max_left), jnp.exp(right - max_right), jnp.exp(low - max_right)
    inv_left = 1.0 / jnp.sum(left, axis=0, keepdims=True)
    inv_right = 1.0 / (jnp.sum(right, axis=0, keepdims=True) + jnp.sum(low, axis=0, keepdims=True))
    return left * inv_left, right * inv_right, low * inv_right


def spread(stat_rows, top, low):
    half = low.shape[0]
    full = dot(stat_rows[:, :half], top, NN)
    return jnp.concatenate([full[:, :half], full[:, half:] + dot(stat_rows[:, half:], low, NN)], axis=1)


def attention_forward_kernel(tabs_ref, qkv_ref, ctx_ref):
    seq_len = qkv_ref.shape[0]
    half = seq_len // 2
    half_cols = qkv_ref.shape[1] // 2
    causal = lax.broadcasted_iota(jnp.int32, (half, half), 0) <= lax.broadcasted_iota(jnp.int32, (half, half), 1)
    first = lax.broadcasted_iota(jnp.int32, (seq_len, 128), 1) < HEAD_DIM
    tabs = (tabs_ref[0], tabs_ref[1], tabs_ref[2])

    @pl.loop(0, ctx_ref.shape[1] // 128, unroll=2)
    def pair_step(pair):
        q_col, k_col, v_col = pair_columns(pair, half_cols)
        query = rotate(qkv_ref[:, q_col].astype(F32), tabs).astype(BF16) * (HEAD_DIM ** -0.5)
        key = rotate(qkv_ref[:, k_col].astype(F32), tabs)
        value_t = qkv_ref[:, v_col].astype(F32).T.astype(BF16)
        outs = []
        for head, keep in enumerate((first, ~first)):
            left, right, low = transposed_probs(jnp.where(keep, key, 0.0).astype(BF16), query, causal)
            top = jnp.concatenate([left.astype(BF16), right.astype(BF16)], axis=1)
            outs.append(spread(value_t[head * HEAD_DIM:(head + 1) * HEAD_DIM], top, low.astype(BF16)))
        ctx_ref[:, pl.ds(pl.multiple_of(pair * 128, 128), 128)] = jnp.concatenate(outs, axis=0).T.astype(BF16)


def attention_backward_kernel(tabs_ref, qkv_ref, gctx_ref, gqkv_ref):
    seq_len = qkv_ref.shape[0]
    half = seq_len // 2
    half_cols = qkv_ref.shape[1] // 2
    scale = HEAD_DIM ** -0.5
    causal = lax.broadcasted_iota(jnp.int32, (half, half), 0) <= lax.broadcasted_iota(jnp.int32, (half, half), 1)
    first = lax.broadcasted_iota(jnp.int32, (seq_len, 128), 1) < HEAD_DIM
    tabs = (tabs_ref[0], tabs_ref[1], tabs_ref[2])

    @pl.loop(0, gctx_ref.shape[1] // 128)
    def pair_step(pair):
        q_col, k_col, v_col = pair_columns(pair, half_cols)
        query = rotate(qkv_ref[:, q_col].astype(F32), tabs).astype(BF16) * scale
        key32 = rotate(qkv_ref[:, k_col].astype(F32), tabs)
        key_t = key32.T.astype(BF16)
        value32 = qkv_ref[:, v_col].astype(F32)
        gctx = gctx_ref[:, pl.ds(pl.multiple_of(pair * 128, 128), 128)]
        gqueries, gkeys, gvalues = [], [], []
        for head, keep in enumerate((first, ~first)):
            value = jnp.where(keep, value32, 0.0).astype(BF16)
            left, right, low = transposed_probs(jnp.where(keep, key32, 0.0).astype(BF16), query, causal)
            gtop = dot(value[:half], gctx, NT)
            glow = dot(value[half:], gctx[half:], NT)
            gleft, gright = gtop[:, :half], gtop[:, half:]
            sum_left = jnp.sum(gleft * left, axis=0, keepdims=True)
            sum_right = jnp.sum(gright * right, axis=0, keepdims=True) + jnp.sum(glow * low, axis=0, keepdims=True)
            top = jnp.concatenate([left.astype(BF16), right.astype(BF16)], axis=1)
            low_b = low.astype(BF16)
            gvalues.append(jnp.concatenate([dot(top, gctx, NN), dot(low_b, gctx[half:], NN)], axis=0))
            dtop = jnp.concatenate([(left * (gleft - sum_left)).astype(BF16), (right * (gright - sum_right)).astype(BF16)], axis=1)
            dlow = (low * (glow - sum_right)).astype(BF16)
            gkeys.append(jnp.concatenate([dot(dtop, query, NN), dot(dlow, query[half:], NN)], axis=0))
            gqueries.append(spread(key_t[head * HEAD_DIM:(head + 1) * HEAD_DIM], dtop, dlow))
        gquery = jnp.concatenate(gqueries, axis=0).T * scale
        gqkv_ref[:, q_col] = rotate_back(gquery, tabs).astype(BF16)
        gqkv_ref[:, k_col] = rotate_back(jnp.where(first, gkeys[0], gkeys[1]), tabs).astype(BF16)
        gqkv_ref[:, v_col] = jnp.where(first, gvalues[0], gvalues[1]).astype(BF16)


def attention_call(kernel, tabs, seq_len, out_cols, n_dots, *arrays):
    tokens = arrays[0].shape[0]
    rows = tokens // seq_len
    width = arrays[0].shape[1] // 3
    heads = width // HEAD_DIM
    return pl.pallas_call(
        kernel,
        grid=(rows,),
        in_specs=[pl.BlockSpec(tabs.shape, lambda i: (0, 0, 0))] + [pl.BlockSpec((seq_len, array.shape[1]), lambda i: (i, 0)) for array in arrays],
        out_specs=pl.BlockSpec((seq_len, out_cols), lambda i: (i, 0)),
        out_shape=jax.ShapeDtypeStruct((tokens, out_cols), BF16),
        compiler_params=pltpu.CompilerParams(dimension_semantics=('arbitrary',), vmem_limit_bytes=48 * 1024 * 1024),
        cost_estimate=pl.CostEstimate(flops=2 * n_dots * rows * heads * seq_len * seq_len * 256, bytes_accessed=2 * tokens * (sum(a.shape[1] for a in arrays) + out_cols), transcendentals=rows * heads * seq_len * seq_len),
    )(tabs, *arrays)


def row_major(values):
    return with_layout_constraint(values, Layout(tuple(range(values.ndim))))


def normalize(hidden):
    hidden_f = hidden.astype(F32)
    center = hidden_f - jnp.mean(hidden_f, axis=-1, keepdims=True)
    inv_std = lax.rsqrt(jnp.mean(center * center, axis=-1, keepdims=True) + LN_EPS)
    return center * inv_std, inv_std


def gelu_parts(pre_act):
    cdf = 0.5 * (1.0 + lax.erf(pre_act * (2.0 ** -0.5)))
    return cdf


def solution(mesh):
    everyone = ('tp', 'pp')

    def device_fn(x_in, g_out, ln1_gain, ln1_bias, w_qkv, b_qkv, w_out, b_out, ln2_gain, ln2_bias, w_up, b_up, w_down, b_down):
        n_stages, tp_size = mesh.shape['pp'], mesh.shape['tp']
        n_dev = n_stages * tp_size
        stage_id = lax.axis_index('pp')
        tp_rank = lax.axis_index('tp')
        rank = tp_rank * n_stages + stage_id
        n_micro, n_rows, seq_len, width = x_in.shape
        own_micro = n_micro // n_dev
        tokens = own_micro * n_rows * seq_len
        tabs = rotary_lanes(seq_len)

        def gather(shard):
            return lax.all_gather(shard, everyone, axis=0, tiled=True)

        def exchange(rows):
            return lax.all_to_all(rows, 'pp', 0, 0, tiled=True)

        heads = w_qkv.shape[2]
        qkv_part = exchange(jnp.transpose(w_qkv[0], (2, 1, 3, 0)).reshape(3 * heads * HEAD_DIM, width))
        out_part = exchange(w_out[0].reshape(heads * HEAD_DIM, width))
        up_part = exchange(jnp.transpose(w_up[0]))
        down_part = exchange(w_down[0])

        def layer(part, index):
            rows = part.shape[0] // n_stages
            return gather(part[index * rows:(index + 1) * rows])

        weights = [tuple(layer(part, index) for part in (qkv_part, out_part, up_part, down_part)) for index in range(n_stages)]

        def small(own, columns):
            return own.reshape(1, columns).astype(F32)

        b_qkv_own = jnp.transpose(b_qkv[0], (1, 0, 2)).reshape(1, -1)
        vec_own = jnp.concatenate([small(b_qkv_own, 3 * heads * HEAD_DIM), small(b_up, b_up.shape[1]), ln1_gain, ln1_bias, ln2_gain, ln2_bias, small(b_out, width), small(b_down, width)], axis=1)
        vec_all = jnp.swapaxes(gather(vec_own).reshape(tp_size, n_stages, -1), 0, 1)
        cut = 0

        def take(columns, split):
            nonlocal cut
            part = vec_all[:, :, cut:cut + columns] if split else vec_all[:, 0, cut:cut + columns]
            cut += columns
            return part.reshape(n_stages, -1)

        bias_qkv = take(3 * heads * HEAD_DIM, True)
        bias_up = take(b_up.shape[1], True)
        gain1, shift1, gain2, shift2, bias_out, bias_down = (take(width, False) for _ in range(6))

        x_own = lax.dynamic_slice_in_dim(x_in, rank * own_micro, own_micro, 0).reshape(tokens, width)
        g_own = lax.dynamic_slice_in_dim(g_out, rank * own_micro, own_micro, 0).reshape(tokens, width).astype(BF16)

        hidden = row_major(x_own)
        saved = []
        for index in range(n_stages):
            all_qkv, all_out, all_up, all_down = weights[index]
            normed, _ = normalize(hidden)
            normed_a = (normed * gain1[index] + shift1[index]).astype(BF16)
            normed_m = (normed * gain2[index] + shift2[index]).astype(BF16)
            qkv_proj = (dot(normed_a, all_qkv, NT) + bias_qkv[index]).astype(BF16)
            context = attention_call(attention_forward_kernel, tabs, seq_len, width, 2, qkv_proj)
            attn_sum = dot(context, all_out, NN)
            pre_act = dot(normed_m, all_up, NT) + bias_up[index]
            hidden_mlp = (pre_act * gelu_parts(pre_act)).astype(BF16)
            mlp_sum = dot(hidden_mlp, all_down, NN)
            saved.append((hidden, normed_a, normed_m, qkv_proj, context, pre_act, hidden_mlp))
            hidden = row_major((hidden.astype(F32) + attn_sum + bias_out[index] + mlp_sum + bias_down[index]).astype(BF16))
        y_out = gather(hidden).reshape(x_in.shape)
        in_flight = [y_out]

        def scatter(full):
            return lax.psum_scatter(full, everyone, scatter_dimension=0, tiled=True)

        grad = row_major(g_own)
        pieces = {name: [None] * n_stages for name in ('qkv', 'out', 'up', 'down')}
        vgrads = [None] * n_stages
        for index in reversed(range(n_stages)):
            hidden, normed_a, normed_m, qkv_proj, context, pre_act, hidden_mlp = saved[index]
            all_qkv, all_out, all_up, all_down = weights[index]
            grad_f = grad.astype(F32)
            grad_context = dot(grad, all_out, NT).astype(BF16)
            grad_qkv = attention_call(attention_backward_kernel, tabs, seq_len, 3 * width, 5, qkv_proj, grad_context)
            d_out = dot(context, grad, TN).astype(BF16)
            d_qkv = dot(grad_qkv, normed_a, TN).astype(BF16)
            if index == 0:
                d_out, d_qkv, grad = lax.optimization_barrier((d_out, d_qkv, grad))
            grad_mlp = dot(grad, all_down, NT)
            slope = gelu_parts(pre_act) + pre_act * jnp.exp(-0.5 * pre_act * pre_act) * ((2.0 * jnp.pi) ** -0.5)
            grad_pre = grad_mlp * slope
            grad_pre_b = grad_pre.astype(BF16)
            d_up = dot(grad_pre_b, normed_m, TN).astype(BF16)
            if index == 0:
                d_up, grad, in_flight = lax.optimization_barrier((d_up, grad, in_flight))
            d_down = dot(hidden_mlp, grad, TN).astype(BF16)
            if index == 0:
                d_down, grad_pre_b, grad_qkv = lax.optimization_barrier((d_down, grad_pre_b, grad_qkv))
            grad_m = dot(grad_pre_b, all_up, NN)
            grad_a = dot(grad_qkv, all_qkv, NN)
            normed, inv_std = normalize(hidden)
            grad_n = grad_a * gain1[index] + grad_m * gain2[index]
            mean_g = jnp.mean(grad_n, axis=-1, keepdims=True)
            mean_gn = jnp.mean(grad_n * normed, axis=-1, keepdims=True)
            vgrads[index] = (jnp.sum(grad_qkv.astype(F32), axis=0), jnp.sum(grad_pre, axis=0), jnp.sum(grad_a * normed, axis=0), jnp.sum(grad_a, axis=0), jnp.sum(grad_m * normed, axis=0), jnp.sum(grad_m, axis=0), jnp.sum(grad_f, axis=0))
            if index > 0:
                grad = row_major((grad_f + inv_std * (grad_n - mean_g - normed * mean_gn)).astype(BF16))
                grad, d_qkv, d_out, d_up, d_down, in_flight = lax.optimization_barrier((grad, d_qkv, d_out, d_up, d_down, in_flight))
            if index < n_stages - 1:
                for name, piece in zip(('qkv', 'out', 'up', 'down'), in_flight):
                    pieces[name][index + 1] = piece
            in_flight = [scatter(full) for full in (d_qkv, d_out, d_up, d_down)]
        for name, piece in zip(('qkv', 'out', 'up', 'down'), in_flight):
            pieces[name][0] = piece

        y_out = jnp.where(stage_id < n_stages, y_out, jnp.zeros_like(y_out))
        y_out, pieces['down'][0] = lax.optimization_barrier((y_out, pieces['down'][0]))
        own = {name: exchange(jnp.concatenate(parts, axis=0)).astype(F32) for name, parts in pieces.items()}
        vec = jnp.stack([jnp.concatenate(parts) for parts in vgrads])
        vec = lax.dynamic_index_in_dim(lax.psum(vec, everyone), stage_id, 0, keepdims=False)
        sizes = [3 * width, b_up.shape[1] * tp_size] + [width] * 5
        vecs, cut = [], 0
        for size in sizes:
            vecs.append(vec[cut:cut + size])
            cut += size
        d_bqkv = lax.dynamic_index_in_dim(vecs[0].reshape(tp_size, 3, heads, HEAD_DIM), tp_rank, 0, keepdims=False)
        d_bup = lax.dynamic_index_in_dim(vecs[1].reshape(tp_size, -1), tp_rank, 0, keepdims=False)
        d_qkv = jnp.transpose(own['qkv'].reshape(3, heads, HEAD_DIM, width), (3, 1, 0, 2))
        grads = (vecs[2], vecs[3], d_qkv, jnp.transpose(d_bqkv, (1, 0, 2)), own['out'].reshape(heads, HEAD_DIM, width), vecs[6], vecs[4], vecs[5], jnp.transpose(own['up']), d_bup, own['down'], vecs[6])
        return tuple([y_out] + [value[None] for value in grads])

    return jax.shard_map(device_fn, mesh=mesh, in_specs=(P('dp'), P('dp')) + STAGE_SPECS, out_specs=(P('dp'),) + GRAD_SPECS, check_vma=False)
```

time: 2530 us -> 2220 us (0.88)
  waiting for transfers between devices: 697 us -> 226 us
  blocking collectives: 15.7 us -> 232 us
  other arithmetic: 206 us -> 127 us
  Pallas kernels: 538 us -> 512 us
    all_gather x5 -> x17, waiting for transfers between devices: 477 us -> 0.1 us  [gather(): return lax.all_gather(shard, everyone, axis=0, tiled=True)]
    all_to_all x0 -> x4, blocking collectives: none -> 219 us  [exchange(): return lax.all_to_all(rows, 'pp', 0, 0, tiled=True)]
    concatenate x4, other arithmetic: 107 us -> 12.6 us  [device_fn(): jnp.concatenate(parts, axis=0)]
    reduce_scatter x4 -> x16, waiting for transfers between devices: 218 us -> 168 us  [scatter(): return lax.psum_scatter(full, everyone, scatter_dimension=0, tiled=True)]
    psum x1, waiting for transfers between devices: 0.02 us -> 46.4 us  [device_fn(): lax.psum(vec, everyone)]
    pallas_call x8, Pallas kernels: 538 us -> 512 us  [attention_call(): pl.pallas_call(kernel, grid=(rows,), in_specs=[pl.BlockSpec(tabs.shape, l...]
  transfers between devices with their start and end apart: 10 -> 38, of which waited for: 7 -> 5; matrix products, arithmetic and copies ran while one was open for 22% -> 52% of each run, Pallas kernels for 2% -> 23%
where the time goes in v1:
time: 2220 us
  matrix products  1010 us (45%)
  Pallas kernels  512 us (23%)
  blocking collectives  232 us (10%)
  waiting for transfers between devices  226 us (10%)
  other arithmetic  127 us (6%)
  local copies, waits for them, and re-layouts  72.3 us (3%)
    dot_general x48, matrix products, dot(): return lax.dot_general(lhs, rhs, dims, preferred_element_type=F32)  1010 us
    pallas_call x8, Pallas kernels, attention_call(): pl.pallas_call(kernel, grid=(rows,), in_specs=[pl.BlockSpec(tabs.shape, l...  512 us
    all_to_all x4, blocking collectives, exchange(): return lax.all_to_all(rows, 'pp', 0, 0, tiled=True)  219 us
    reduce_scatter x16, waiting for transfers between devices, scatter(): return lax.psum_scatter(full, everyone, scatter_dimension=0, tiled=True)  168 us
    psum x1, waiting for transfers between devices, device_fn(): lax.psum(vec, everyone)  46.4 us
  transfers between devices with their start and end apart: 38, of which 5 were waited for; matrix products, arithmetic and copies ran while one was open for 52% of the time, Pallas kernels for 23%

profile of v1, /device:TPU:0, one launch (start us, length us, event | category | flops | bytes accessed | tf_op | source)
XLA Modules:
  0.0 2215.3 jit_solution(15569171462660280768)
XLA Ops:
  9.7 41.3 %all_to_all.72 = bf16[4,384,1024]{2,1,0:T(8,128)(2,1)S(1)} all-to-all(bf16[4,384,1024]{2,1,0:T(8,128)(2,1)S(1)} %bitcast.275), channel_id=1, replica_groups=mesh['dp'=1,'tp'=2,'pp'=4] {'pp'}, dimensions={0} | all-to-all | bytes 6291456 | tf_op jit(solution)/shard_map/all_to_all | solution.py:185
  85.3 67.1 %all_to_all.74 = bf16[4,512,1024]{2,1,0:T(8,128)(2,1)S(1)} all-to-all(bf16[4,512,1024]{2,1,0:T(8,128)(2,1)} %bitcast.270), channel_id=1, replica_groups=mesh['dp'=1,'tp'=2,'pp'=4] {'pp'}, dimensions={0} | all-to-all | bytes 8388608 | tf_op jit(solution)/shard_map/all_to_all | solution.py:185
  154.6 85.6 %all_to_all.75 = bf16[4,512,1024]{2,1,0:T(8,128)(2,1)S(1)} all-to-all(bf16[4,512,1024]{2,1,0:T(8,128)(2,1)} %bitcast.280), channel_id=1, replica_groups=mesh['dp'=1,'tp'=2,'pp'=4] {'pp'}, dimensions={0} | all-to-all | bytes 8388608 | tf_op jit(solution)/shard_map/all_to_all | solution.py:185
  296.9 47.8 %shard_map.237 = bf16[2048,1024]{1,0:T(8,128)(2,1)S(1)} custom-call(f32[3,256,128]{2,1,0:T(8,128)S(1)} %pad_maximum_fusion.4.tabs_ref, bf16[2048,3072]{1,0:T(8,128)(2,1)} %add_convert_fusion.3.qkv_ref), custom_call_target="tpu_custom_call" | custom-call | flops 8589934592 | bytes 16777216 | tf_op jit(solution)/shard_map/pallas_call | solution.py:140
  357.8 29.3 %multiply_convert_fusion.3 = (bf16[2048,4096]{1,0:T(8,128)(2,1)}, f32[2048,4096]{1,0:T(8,128)}) fusion(f32[4096]{0:T(1024)S(1)} %bitcast.297, bf16[2048,1024]{1,0:T(8,128)(2,1)} %get-tuple-element.157, bf16[1,4096,1024]{2,1,0:T(8,128)(2,1)} %all-gather.41.cloned.1.call-done), kind=kOutput, calls=%fused_computation.30 | convolution fusion | flops 17230200832 | bytes 62930944 | tf_op jit(solution)/shard_map/dot_general | solution.py:22
  436.8 47.8 %shard_map.238 = bf16[2048,1024]{1,0:T(8,128)(2,1)S(1)} custom-call(f32[3,256,128]{2,1,0:T(8,128)S(1)} %pad_maximum_fusion.4.tabs_ref, bf16[2048,3072]{1,0:T(8,128)(2,1)} %add_convert_fusion.2.qkv_ref), custom_call_target="tpu_custom_call" | custom-call | flops 8589934592 | bytes 16777216 | tf_op jit(solution)/shard_map/pallas_call | solution.py:140
  497.5 30.7 %multiply_convert_fusion.2 = (bf16[2048,4096]{1,0:T(8,128)(2,1)}, f32[2048,4096]{1,0:T(8,128)}) fusion(f32[4096]{0:T(1024)S(1)} %bitcast.299, bf16[1,4096,1024]{2,1,0:T(8,128)(2,1)} %all-gather.49.cloned.1.call-done, bf16[2048,1024]{1,0:T(8,128)(2,1)} %copy-done.10, f32[1024]{0:T(1024)S(1)} %bitcast.309, f32[1024]{0:T(1024)S(1)} %bitcast.311, ...), kind=kOutput, calls=%fused_computation.28 | convolution fusion | flops 17242783744 | bytes 62955520 | tf_op jit(solution)/shard_map/dot_general | solution.py:22
  578.4 47.8 %shard_map.239 = bf16[2048,1024]{1,0:T(8,128)(2,1)S(1)} custom-call(f32[3,256,128]{2,1,0:T(8,128)S(1)} %pad_maximum_fusion.4.tabs_ref, bf16[2048,3072]{1,0:T(8,128)(2,1)} %add_convert_fusion.1.qkv_ref), custom_call_target="tpu_custom_call" | custom-call | flops 8589934592 | bytes 16777216 | tf_op jit(solution)/shard_map/pallas_call | solution.py:140
  639.1 30.6 %multiply_convert_fusion.1 = (bf16[2048,4096]{1,0:T(8,128)(2,1)}, f32[2048,4096]{1,0:T(8,128)}) fusion(f32[4096]{0:T(1024)S(1)} %bitcast.301, bf16[1,4096,1024]{2,1,0:T(8,128)(2,1)} %all-gather.57.cloned.1.call-done, bf16[2048,1024]{1,0:T(8,128)(2,1)} %copy-done.12, f32[1024]{0:T(1024)S(1)} %bitcast.319, f32[1024]{0:T(1024)S(1)} %bitcast.321, ...), kind=kOutput, calls=%fused_computation.26 | convolution fusion | flops 17242783744 | bytes 62955520 | tf_op jit(solution)/shard_map/dot_general | solution.py:22
  720.4 47.8 %shard_map.240 = bf16[2048,1024]{1,0:T(8,128)(2,1)S(1)} custom-call(f32[3,256,128]{2,1,0:T(8,128)S(1)} %pad_maximum_fusion.4.tabs_ref, bf16[2048,3072]{1,0:T(8,128)(2,1)} %add_convert_fusion.qkv_ref), custom_call_target="tpu_custom_call" | custom-call | flops 8589934592 | bytes 16777216 | tf_op jit(solution)/shard_map/pallas_call | solution.py:140
  781.1 30.8 %multiply_convert_fusion = (bf16[2048,4096]{1,0:T(8,128)(2,1)}, f32[2048,4096]{1,0:T(8,128)}) fusion(f32[4096]{0:T(1024)S(1)} %bitcast.303, bf16[1,4096,1024]{2,1,0:T(8,128)(2,1)} %all-gather.65.cloned.1.call-done, bf16[2048,1024]{1,0:T(8,128)(2,1)} %copy-done.16, f32[1024]{0:T(1024)S(1)} %bitcast.329, f32[1024]{0:T(1024)S(1)} %bitcast.331, ...), kind=kOutput, calls=%fused_computation.24 | convolution fusion | flops 17242783744 | bytes 62955520 | tf_op jit(solution)/shard_map/dot_general | solution.py:22
  846.6 80.3 %shard_map.241 = bf16[2048,3072]{1,0:T(8,128)(2,1)} custom-call(f32[3,256,128]{2,1,0:T(8,128)S(1)} %pad_maximum_fusion.4.tabs_ref, bf16[2048,3072]{1,0:T(8,128)(2,1)} %add_convert_fusion.qkv_ref, bf16[2048,1024]{1,0:T(8,128)(2,1)S(1)} %convolution_convert_fusion.12.gctx_ref), custom_call_target="tpu_custom_call" | custom-call | flops 21474836480 | bytes 29360128 | tf_op jit(solution)/shard_map/pallas_call | solution.py:140
  946.2 37.1 %fusion.220 = (f32[4096]{0:T(1024)}, bf16[2048,4096]{1,0:T(8,128)(2,1)}) fusion(f32[2048,4096]{1,0:T(8,128)} %get-tuple-element.236, f32[4096]{0:T(1024)S(1)} %bitcast.304, bf16[2048,1024]{1,0:T(8,128)(2,1)S(1)} %bitcast.272, bf16[1,4096,1024]{2,1,0:T(8,128)(2,1)} %all-gather.67.cloned.1.call-done), kind=kOutput, calls=%fused_computation.325 | convolution fusion | flops 17280528384 | bytes 62947328 | tf_op jit(solution)/shard_map/dot_general | solution.py:22
  1101.0 80.1 %shard_map.242 = bf16[2048,3072]{1,0:T(8,128)(2,1)} custom-call(f32[3,256,128]{2,1,0:T(8,128)S(1)} %pad_maximum_fusion.4.tabs_ref, bf16[2048,3072]{1,0:T(8,128)(2,1)} %add_convert_fusion.1.qkv_ref, bf16[2048,1024]{1,0:T(8,128)(2,1)S(1)} %convolution_convert_fusion.11.gctx_ref), custom_call_target="tpu_custom_call" | custom-call | flops 21474836480 | bytes 29360128 | tf_op jit(solution)/shard_map/pallas_call | solution.py:140
  1199.7 37.5 %fusion.221 = (f32[4096]{0:T(1024)}, bf16[2048,4096]{1,0:T(8,128)(2,1)}) fusion(f32[2048,4096]{1,0:T(8,128)} %get-tuple-element.232, f32[4096]{0:T(1024)S(1)} %bitcast.302, bf16[2048,1024]{1,0:T(8,128)(2,1)S(1)} %copy-done.21, bf16[1,4096,1024]{2,1,0:T(8,128)(2,1)} %all-gather.59.cloned.1.call-done), kind=kOutput, calls=%fused_computation.326 | convolution fusion | flops 17280528384 | bytes 62947328 | tf_op jit(solution)/shard_map/dot_general | solution.py:22
  1361.6 80.2 %shard_map.243 = bf16[2048,3072]{1,0:T(8,128)(2,1)} custom-call(f32[3,256,128]{2,1,0:T(8,128)S(1)} %pad_maximum_fusion.4.tabs_ref, bf16[2048,3072]{1,0:T(8,128)(2,1)} %add_convert_fusion.2.qkv_ref, bf16[2048,1024]{1,0:T(8,128)(2,1)S(1)} %convolution_convert_fusion.10.gctx_ref), custom_call_target="tpu_custom_call" | custom-call | flops 21474836480 | bytes 29360128 | tf_op jit(solution)/shard_map/pallas_call | solution.py:140
  1460.6 37.3 %fusion.222 = (f32[4096]{0:T(1024)}, bf16[2048,4096]{1,0:T(8,128)(2,1)}) fusion(f32[2048,4096]{1,0:T(8,128)} %get-tuple-element.228, f32[4096]{0:T(1024)S(1)} %bitcast.300, bf16[2048,1024]{1,0:T(8,128)(2,1)S(1)} %copy-done.19, bf16[1,4096,1024]{2,1,0:T(8,128)(2,1)} %all-gather.51.cloned.1.call-done), kind=kOutput, calls=%fused_computation.327 | convolution fusion | flops 17280528384 | bytes 62947328 | tf_op jit(solution)/shard_map/dot_general | solution.py:22
  1632.9 80.2 %shard_map.244 = bf16[2048,3072]{1,0:T(8,128)(2,1)} custom-call(f32[3,256,128]{2,1,0:T(8,128)S(1)} %pad_maximum_fusion.4.tabs_ref, bf16[2048,3072]{1,0:T(8,128)(2,1)} %add_convert_fusion.3.qkv_ref, bf16[2048,1024]{1,0:T(8,128)(2,1)S(1)} %copy-done.8), custom_call_target="tpu_custom_call" | custom-call | flops 21474836480 | bytes 29360128 | tf_op jit(solution)/shard_map/pallas_call | solution.py:140
  1732.2 37.1 %fusion.210 = (f32[4096]{0:T(1024)}, bf16[2048,4096]{1,0:T(8,128)(2,1)S(1)}) fusion(f32[2048,4096]{1,0:T(8,128)} %get-tuple-element.224, f32[4096]{0:T(1024)S(1)} %bitcast.298, bf16[2048,1024]{1,0:T(8,128)(2,1)} %get-tuple-element.66, bf16[1,4096,1024]{2,1,0:T(8,128)(2,1)} %all-gather.43.cloned.1.call-done), kind=kOutput, calls=%fused_computation.315 | convolution fusion | flops 17280528384 | bytes 62947328 | tf_op jit(solution)/shard_map/dot_general | solution.py:22
  1794.8 42.7 %reduce-scatter.39.cloned.1.call-done = bf16[512,1024]{1,0:T(8,128)(2,1)} async-done(((bf16[4096,1024]{1,0:T(8,128)(2,1)}), bf16[512,1024]{1,0:T(8,128)(2,1)}) %reduce-scatter.39.cloned.1.call-update) | async-done | bytes 1048592 | tf_op jit(solution)/shard_map/reduce_scatter | solution.py:239
  1967.2 56.8 %reduce-scatter.47.cloned.1.call-done = bf16[512,1024]{1,0:T(8,128)(2,1)} async-done(((bf16[4096,1024]{1,0:T(8,128)(2,1)}), bf16[512,1024]{1,0:T(8,128)(2,1)}) %reduce-scatter.47.cloned.1.call-update) | async-done | bytes 1048592 | tf_op jit(solution)/shard_map/reduce_scatter | solution.py:239
  2032.6 27.8 %fusion.199 = (f32[1024]{0:T(1024)S(1)}, f32[1024]{0:T(1024)S(1)}, f32[1024]{0:T(1024)S(1)}, f32[1024]{0:T(1024)S(1)}) fusion(f32[2048]{0:T(1024)S(1)} %copy-done.39, f32[2048]{0:T(1024)S(1)} %copy-done.31, bf16[2,4,256,1024]{3,2,1,0:T(8,128)(2,1)} %copy-done.9, f32[2048,1024]{1,0:T(8,128)} %fusion.161, bf16[2048,4096]{1,0:T(8,128)(2,1)} %copy-done.119, ...), kind=kOutput, calls=%fused_computation.304 | convolution fusion | flops 17198743552 | bytes 37781504 | tf_op jit(solution)/shard_map/dot_general | solution.py:22
  2062.8 53.1 %reduce-scatter.41.cloned.1.call-done = bf16[512,1024]{1,0:T(8,128)(2,1)} async-done(((bf16[4096,1024]{1,0:T(8,128)(2,1)}), bf16[512,1024]{1,0:T(8,128)(2,1)}) %reduce-scatter.41.cloned.1.call-update) | async-done | bytes 1048592 | tf_op jit(solution)/shard_map/reduce_scatter | solution.py:239
  2127.1 46.4 %all-reduce.2.cloned.1.call-done = f32[4,12288]{1,0:T(4,128)} async-done(((f32[4,12288]{1,0:T(4,128)}), f32[4,12288]{1,0:T(4,128)}) %all-reduce.2.cloned.1.call-update) | async-done | bytes 196624 | tf_op jit(solution)/shard_map/psum | solution.py:285
  (512 shorter events, 995.0 us)
Async XLA Ops:
  7.2 270.2 %all-gather.37.cloned.1.call-start = ((), (), s32[]{:S(2)}) async-start(), calls=%async_computation.42 | async-start | bytes 7077888 | tf_op jit(solution)/shard_map/all_gather | solution.py:182
  52.7 294.1 %all-gather.39.cloned.1.call-start = ((), (), s32[]{:S(2)}) async-start(), calls=%async_computation.43 | async-start | bytes 2359296 | tf_op jit(solution)/shard_map/all_gather | solution.py:182
  79.0 278.7 %all-gather.41.cloned.1.call-start = ((), (), s32[]{:S(2)}) async-start(), calls=%async_computation.44 | async-start | bytes 9437184 | tf_op jit(solution)/shard_map/all_gather | solution.py:182
  243.5 254.0 %all-gather.49.cloned.1.call-start = ((), (), s32[]{:S(2)}) async-start(), calls=%async_computation.48 | async-start | bytes 9437184 | tf_op jit(solution)/shard_map/all_gather | solution.py:182
  244.3 284.0 %all-gather.51.cloned.1.call-start = ((), (), s32[]{:S(2)}) async-start(), calls=%async_computation.49 | async-start | bytes 9437184 | tf_op jit(solution)/shard_map/all_gather | solution.py:182
  245.0 312.2 %all-gather.53.cloned.1.call-start = ((), (), s32[]{:S(2)}) async-start(), calls=%async_computation.50 | async-start | bytes 7077888 | tf_op jit(solution)/shard_map/all_gather | solution.py:182
  245.8 382.5 %all-gather.55.cloned.1.call-start = ((), (), s32[]{:S(2)}) async-start(), calls=%async_computation.51 | async-start | bytes 2359296 | tf_op jit(solution)/shard_map/all_gather | solution.py:182
  246.4 392.7 %all-gather.57.cloned.1.call-start = ((), (), s32[]{:S(2)}) async-start(), calls=%async_computation.52 | async-start | bytes 9437184 | tf_op jit(solution)/shard_map/all_gather | solution.py:182
  247.1 422.6 %all-gather.59.cloned.1.call-start = ((), (), s32[]{:S(2)}) async-start(), calls=%async_computation.53 | async-start | bytes 9437184 | tf_op jit(solution)/shard_map/all_gather | solution.py:182
  247.7 450.4 %all-gather.61.cloned.1.call-start = ((), (), s32[]{:S(2)}) async-start(), calls=%async_computation.54 | async-start | bytes 7077888 | tf_op jit(solution)/shard_map/all_gather | solution.py:182
  248.4 521.8 %all-gather.63.cloned.1.call-start = ((), (), s32[]{:S(2)}) async-start(), calls=%async_computation.55 | async-start | bytes 2359296 | tf_op jit(solution)/shard_map/all_gather | solution.py:182
  249.0 532.0 %all-gather.65.cloned.1.call-start = ((), (), s32[]{:S(2)}) async-start(), calls=%async_computation.56 | async-start | bytes 9437184 | tf_op jit(solution)/shard_map/all_gather | solution.py:182
  249.6 562.3 %all-gather.67.cloned.1.call-start = ((), (), s32[]{:S(2)}) async-start(), calls=%async_computation.57 | async-start | bytes 9437184 | tf_op jit(solution)/shard_map/all_gather | solution.py:182
  277.1 815.1 %all-gather.35.cloned.1.call-start = ((), (), s32[]{:S(2)}) async-start(), calls=%async_computation.24 | async-start | bytes 37748736 | tf_op jit(solution)/shard_map/all_gather | solution.py:182
  837.4 515.5 %reduce-scatter.19.cloned.1.call-start = ((), (), s32[]{:S(2)}) async-start(), calls=%async_computation.26 | async-start | bytes 2359296 | tf_op jit(solution)/shard_map/reduce_scatter | solution.py:239
  1092.3 260.6 %reduce-scatter.17.cloned.1.call-start = ((), (), s32[]{:S(2)}) async-start(), calls=%async_computation.25 | async-start | bytes 7077888 | tf_op jit(solution)/shard_map/reduce_scatter | solution.py:239
  1093.0 259.9 %reduce-scatter.21.cloned.1.call-start = ((), (), s32[]{:S(2)}) async-start(), calls=%async_computation.27 | async-start | bytes 9437184 | tf_op jit(solution)/shard_map/reduce_scatter | solution.py:239
  1263.0 350.5 %reduce-scatter.27.cloned.1.call-start = ((), (), s32[]{:S(2)}) async-start(), calls=%async_computation.30 | async-start | bytes 2359296 | tf_op jit(solution)/shard_map/reduce_scatter | solution.py:239
  1353.0 260.6 %reduce-scatter.25.cloned.1.call-start = ((), (), s32[]{:S(2)}) async-start(), calls=%async_computation.29 | async-start | bytes 7077888 | tf_op jit(solution)/shard_map/reduce_scatter | solution.py:239
  1353.7 259.8 %reduce-scatter.29.cloned.1.call-start = ((), (), s32[]{:S(2)}) async-start(), calls=%async_computation.31 | async-start | bytes 9437184 | tf_op jit(solution)/shard_map/reduce_scatter | solution.py:239
  1523.6 271.2 %reduce-scatter.35.cloned.1.call-start = ((), (), s32[]{:S(2)}) async-start(), calls=%async_computation.34 | async-start | bytes 2359296 | tf_op jit(solution)/shard_map/reduce_scatter | solution.py:239
  1615.7 292.4 %reduce-scatter.45.cloned.1.call-start = ((), (), s32[]{:S(2)}) async-start(), calls=%async_computation.40 | async-start | bytes 2359296 | tf_op jit(solution)/shard_map/reduce_scatter | solution.py:239
  1732.1 291.9 %reduce-scatter.47.cloned.1.call-start = ((), (), s32[]{:S(2)}) async-start(), calls=%async_computation.41 | async-start | bytes 9437184 | tf_op jit(solution)/shard_map/reduce_scatter | solution.py:239
  1837.7 278.2 %reduce-scatter.41.cloned.1.call-start = ((), (), s32[]{:S(2)}) async-start(), calls=%async_computation.37 | async-start | bytes 9437184 | tf_op jit(solution)/shard_map/reduce_scatter | solution.py:239
  (138 other events, 5173.3 us)
Sparse Core Ops, SparseCore 0:
  52.8 54.5 all-gather.36
  154.6 81.7 all-gather.40
  242.5 50.3 all-gather.42
  360.9 48.6 all-gather.48
  411.5 48.6 all-gather.50
  462.0 40.1 all-gather.52
  528.5 48.6 all-gather.56
  578.9 48.8 all-gather.58
  695.6 48.6 all-gather.64
  746.0 48.7 all-gather.66
  837.5 156.4 all-gather.34
  1130.1 53.4 reduce-scatter.16
  1187.3 63.1 reduce-scatter.20
  1263.2 63.9 reduce-scatter.22
  1389.8 53.4 reduce-scatter.24
  1446.5 63.1 reduce-scatter.28
  1523.7 63.6 reduce-scatter.30
  1650.3 53.4 reduce-scatter.32
  1707.8 63.1 reduce-scatter.36
  1774.4 63.1 reduce-scatter.38
  1876.7 61.4 reduce-scatter.42
  1942.2 81.6 reduce-scatter.46
  2027.2 88.6 reduce-scatter.40
  2128.9 44.6 all-reduce.1
  (10 shorter events, 309.3 us)

commit v2 on v1

--- a/solution.py
+++ b/solution.py
@@ -73,24 +73,25 @@
 
 def attention_forward_kernel(tabs_ref, qkv_ref, ctx_ref):
     seq_len = qkv_ref.shape[0]
-    half = seq_len // 2
     half_cols = qkv_ref.shape[1] // 2
-    causal = lax.broadcasted_iota(jnp.int32, (half, half), 0) <= lax.broadcasted_iota(jnp.int32, (half, half), 1)
+    causal = lax.broadcasted_iota(jnp.int32, (seq_len, seq_len), 0) >= lax.broadcasted_iota(jnp.int32, (seq_len, seq_len), 1)
     first = lax.broadcasted_iota(jnp.int32, (seq_len, 128), 1) < HEAD_DIM
     tabs = (tabs_ref[0], tabs_ref[1], tabs_ref[2])
 
     @pl.loop(0, ctx_ref.shape[1] // 128, unroll=2)
     def pair_step(pair):
         q_col, k_col, v_col = pair_columns(pair, half_cols)
-        query = rotate(qkv_ref[:, q_col].astype(F32), tabs).astype(BF16) * (HEAD_DIM ** -0.5)
-        key = rotate(qkv_ref[:, k_col].astype(F32), tabs)
-        value_t = qkv_ref[:, v_col].astype(F32).T.astype(BF16)
+        query = rotate(qkv_ref[:, q_col].astype(F32), tabs) * (HEAD_DIM ** -0.5)
+        key = rotate(qkv_ref[:, k_col].astype(F32), tabs).astype(BF16)
+        value = qkv_ref[:, v_col]
         outs = []
-        for head, keep in enumerate((first, ~first)):
-            left, right, low = transposed_probs(jnp.where(keep, key, 0.0).astype(BF16), query, causal)
-            top = jnp.concatenate([left.astype(BF16), right.astype(BF16)], axis=1)
-            outs.append(spread(value_t[head * HEAD_DIM:(head + 1) * HEAD_DIM], top, low.astype(BF16)))
-        ctx_ref[:, pl.ds(pl.multiple_of(pair * 128, 128), 128)] = jnp.concatenate(outs, axis=0).T.astype(BF16)
+        for keep in (first, ~first):
+            scores = dot(jnp.where(keep, query, 0.0).astype(BF16), key, NT)
+            scores = jnp.where(causal, scores, -1e30)
+            expo = jnp.exp(scores - jnp.max(scores, axis=1, keepdims=True))
+            probs = expo * (1.0 / jnp.sum(expo, axis=1, keepdims=True))
+            outs.append(dot(probs.astype(BF16), value, NN))
+        ctx_ref[:, pl.ds(pl.multiple_of(pair * 128, 128), 128)] = jnp.where(first, outs[0], outs[1]).astype(BF16)
 
 
 def attention_backward_kernel(tabs_ref, qkv_ref, gctx_ref, gqkv_ref):
@@ -185,16 +186,13 @@
             return lax.all_to_all(rows, 'pp', 0, 0, tiled=True)
 
         heads = w_qkv.shape[2]
-        qkv_part = exchange(jnp.transpose(w_qkv[0], (2, 1, 3, 0)).reshape(3 * heads * HEAD_DIM, width))
-        out_part = exchange(w_out[0].reshape(heads * HEAD_DIM, width))
+
+        def gather_stages(shard):
+            return lax.all_gather(shard, ('pp', 'tp'), axis=0, tiled=True).reshape(n_stages, -1, width)
+
+        qkv_stages = gather_stages(jnp.transpose(w_qkv[0], (2, 1, 3, 0)).reshape(3 * heads * HEAD_DIM, width))
+        out_stages = gather_stages(w_out[0].reshape(heads * HEAD_DIM, width))
         up_part = exchange(jnp.transpose(w_up[0]))
-        down_part = exchange(w_down[0])
-
-        def layer(part, index):
-            rows = part.shape[0] // n_stages
-            return gather(part[index * rows:(index + 1) * rows])
-
-        weights = [tuple(layer(part, index) for part in (qkv_part, out_part, up_part, down_part)) for index in range(n_stages)]
 
         def small(own, columns):
             return own.reshape(1, columns).astype(F32)
@@ -218,12 +216,25 @@
         g_own = lax.dynamic_slice_in_dim(g_out, rank * own_micro, own_micro, 0).reshape(tokens, width).astype(BF16)
 
         hidden = row_major(x_own)
+
+        def normed_pair(hidden, index):
+            normed, _ = normalize(hidden)
+            return (normed * gain1[index] + shift1[index]).astype(BF16), (normed * gain2[index] + shift2[index]).astype(BF16)
+
+        down_rows, tabs, normed_first, bias_qkv, bias_up = lax.optimization_barrier((w_down[0], tabs, normed_pair(hidden, 0), bias_qkv, bias_up))
+        down_part = exchange(down_rows)
+        qkv_stages, up_part, down_part = lax.optimization_barrier((qkv_stages, up_part, down_part))
+
+        def layer(part, index):
+            rows = part.shape[0] // n_stages
+            return gather(part[index * rows:(index + 1) * rows])
+
+        weights = [(qkv_stages[index], out_stages[index], layer(up_part, index), layer(down_part, index)) for index in range(n_stages)]
+
         saved = []
         for index in range(n_stages):
             all_qkv, all_out, all_up, all_down = weights[index]
-            normed, _ = normalize(hidden)
-            normed_a = (normed * gain1[index] + shift1[index]).astype(BF16)
-            normed_m = (normed * gain2[index] + shift2[index]).astype(BF16)
+            normed_a, normed_m = normed_pair(hidden, index) if index else normed_first
             qkv_proj = (dot(normed_a, all_qkv, NT) + bias_qkv[index]).astype(BF16)
             context = attention_call(attention_forward_kernel, tabs, seq_len, width, 2, qkv_proj)
             attn_sum = dot(context, all_out, NN)
@@ -239,28 +250,32 @@
             return lax.psum_scatter(full, everyone, scatter_dimension=0, tiled=True)
 
         grad = row_major(g_own)
-        pieces = {name: [None] * n_stages for name in ('qkv', 'out', 'up', 'down')}
+        pieces = {name: [None] * n_stages for name in ('down', 'up', 'qkv')}
+        d_outs = [None] * n_stages
         vgrads = [None] * n_stages
         for index in reversed(range(n_stages)):
             hidden, normed_a, normed_m, qkv_proj, context, pre_act, hidden_mlp = saved[index]
             all_qkv, all_out, all_up, all_down = weights[index]
             grad_f = grad.astype(F32)
-            grad_context = dot(grad, all_out, NT).astype(BF16)
-            grad_qkv = attention_call(attention_backward_kernel, tabs, seq_len, 3 * width, 5, qkv_proj, grad_context)
-            d_out = dot(context, grad, TN).astype(BF16)
-            d_qkv = dot(grad_qkv, normed_a, TN).astype(BF16)
-            if index == 0:
-                d_out, d_qkv, grad = lax.optimization_barrier((d_out, d_qkv, grad))
+            d_down = dot(hidden_mlp, grad, TN).astype(BF16)
+            d_down, grad = lax.optimization_barrier((d_down, grad))
+            pieces['down'][index] = scatter(d_down)
             grad_mlp = dot(grad, all_down, NT)
             slope = gelu_parts(pre_act) + pre_act * jnp.exp(-0.5 * pre_act * pre_act) * ((2.0 * jnp.pi) ** -0.5)
             grad_pre = grad_mlp * slope
             grad_pre_b = grad_pre.astype(BF16)
             d_up = dot(grad_pre_b, normed_m, TN).astype(BF16)
-            if index == 0:
-                d_up, grad, in_flight = lax.optimization_barrier((d_up, grad, in_flight))
-            d_down = dot(hidden_mlp, grad, TN).astype(BF16)
-            if index == 0:
-                d_down, grad_pre_b, grad_qkv = lax.optimization_barrier((d_down, grad_pre_b, grad_qkv))
+            d_up, grad = lax.optimization_barrier((d_up, grad))
+            pieces['up'][index] = scatter(d_up)
+            grad_context = dot(grad, all_out, NT).astype(BF16)
+            grad_qkv = attention_call(attention_backward_kernel, tabs, seq_len, 3 * width, 5, qkv_proj, grad_context)
+            d_out = dot(context, grad, TN).astype(BF16)
+            d_qkv = dot(grad_qkv, normed_a, TN).astype(BF16)
+            d_qkv, d_outs[index], grad_qkv, grad_pre_b, in_flight = lax.optimization_barrier((d_qkv, d_out, grad_qkv, grad_pre_b, in_flight))
+            if index < n_stages - 1:
+                pieces['down'][index + 1], pieces['up'][index + 1], pieces['qkv'][index + 1] = in_flight
+            pieces['qkv'][index] = scatter(d_qkv)
+            in_flight = [pieces[name][index] for name in ('down', 'up', 'qkv')]
             grad_m = dot(grad_pre_b, all_up, NN)
             grad_a = dot(grad_qkv, all_qkv, NN)
             normed, inv_std = normalize(hidden)
@@ -270,19 +285,14 @@
             vgrads[index] = (jnp.sum(grad_qkv.astype(F32), axis=0), jnp.sum(grad_pre, axis=0), jnp.sum(grad_a * normed, axis=0), jnp.sum(grad_a, axis=0), jnp.sum(grad_m * normed, axis=0), jnp.sum(grad_m, axis=0), jnp.sum(grad_f, axis=0))
             if index > 0:
                 grad = row_major((grad_f + inv_std * (grad_n - mean_g - normed * mean_gn)).astype(BF16))
-                grad, d_qkv, d_out, d_up, d_down, in_flight = lax.optimization_barrier((grad, d_qkv, d_out, d_up, d_down, in_flight))
-            if index < n_stages - 1:
-                for name, piece in zip(('qkv', 'out', 'up', 'down'), in_flight):
-                    pieces[name][index + 1] = piece
-            in_flight = [scatter(full) for full in (d_qkv, d_out, d_up, d_down)]
-        for name, piece in zip(('qkv', 'out', 'up', 'down'), in_flight):
-            pieces[name][0] = piece
+        own_out = lax.psum_scatter(jnp.concatenate(d_outs, axis=0), ('pp', 'tp'), scatter_dimension=0, tiled=True)
 
         y_out = jnp.where(stage_id < n_stages, y_out, jnp.zeros_like(y_out))
-        y_out, pieces['down'][0] = lax.optimization_barrier((y_out, pieces['down'][0]))
+        y_out, pieces['qkv'][0] = lax.optimization_barrier((y_out, pieces['qkv'][0]))
         own = {name: exchange(jnp.concatenate(parts, axis=0)).astype(F32) for name, parts in pieces.items()}
-        vec = jnp.stack([jnp.concatenate(parts) for parts in vgrads])
-        vec = lax.dynamic_index_in_dim(lax.psum(vec, everyone), stage_id, 0, keepdims=False)
+        own['out'] = own_out.astype(F32)
+        vec = jnp.sum(exchange(jnp.stack([jnp.concatenate(parts) for parts in vgrads])), axis=0)
+        vec = jnp.sum(lax.all_gather(vec, 'tp', axis=0), axis=0)
         sizes = [3 * width, b_up.shape[1] * tp_size] + [width] * 5
         vecs, cut = [], 0
         for size in sizes:

time: 2220 us -> 2040 us (0.919)
  blocking collectives: 232 us -> 103 us
  waiting for transfers between devices: 226 us -> 184 us
  Pallas kernels: 512 us -> 483 us
    all_to_all x4 -> x0, blocking collectives: 219 us -> none  [exchange(): return lax.all_to_all(rows, 'pp', 0, 0, tiled=True)]
    reduce_scatter x16 -> x12, waiting for transfers between devices: 168 us -> 0.11 us  [scatter(): return lax.psum_scatter(full, everyone, scatter_dimension=0, tiled=True)]
    all_to_all x4 -> x6, waiting for transfers between devices: 0.01 us -> 165 us  [exchange(): return lax.all_to_all(rows, 'pp', 0, 0, tiled=True)]
    all_gather x1, blocking collectives: 13.2 us -> 98 us  [gather(): return lax.all_gather(shard, everyone, axis=0, tiled=True)]
    psum x1 -> x0, waiting for transfers between devices: 46.4 us -> none  [device_fn(): lax.psum(vec, everyone)]
    pallas_call x8, Pallas kernels: 512 us -> 483 us  [attention_call(): pl.pallas_call(kernel, grid=(rows,), in_specs=[pl.BlockSpec(tabs.shape, l...]
  transfers between devices with their start and end apart: 38 -> 30, of which waited for: 5 -> 6; matrix products, arithmetic and copies ran while one was open for 52% -> 57% of each run, Pallas kernels for 23% -> 24%
where the time goes in v2:
time: 2040 us; the launch traced here: 2030 us
  matrix products  1010 us (50%)
  Pallas kernels  483 us (24%)
  waiting for transfers between devices  184 us (9%)
  other arithmetic  121 us (6%)
  blocking collectives  103 us (5%)
  local copies, waits for them, and re-layouts  83.3 us (4%)
  starting transfers between devices  28.6 us (1%)
    dot_general x48, matrix products, dot(): return lax.dot_general(lhs, rhs, dims, preferred_element_type=F32)  1010 us
    pallas_call x8, Pallas kernels, attention_call(): pl.pallas_call(kernel, grid=(rows,), in_specs=[pl.BlockSpec(tabs.shape, l...  483 us
    all_to_all x6, waiting for transfers between devices, exchange(): return lax.all_to_all(rows, 'pp', 0, 0, tiled=True)  165 us
    all_gather x1, blocking collectives, gather(): return lax.all_gather(shard, everyone, axis=0, tiled=True)  98 us
  transfers between devices with their start and end apart: 30, of which 6 were waited for; matrix products, arithmetic and copies ran while one was open for 57% of the time, Pallas kernels for 24%

profile of v2, /device:TPU:0, one launch (start us, length us, event | category | flops | bytes accessed | tf_op | source)
XLA Modules:
  0.0 2029.9 jit_solution(11314049588386248751)
XLA Ops:
  30.4 98.0 %all-gather.1 = f32[8,1,9728]{2,1,0:T(1,128)S(1)} all-gather(f32[1,1,9728]{2,1,0:T(1,128)S(1)} %bitcast.225), channel_id=1, replica_groups=mesh['dp'=1,'tp'=2,'pp'=4] {'tp','pp'}, dimensions={0}, use_global_device_ids=true | all-gather | bytes 350208 | tf_op jit(solution)/shard_map/all_gather | solution.py:183
  151.3 75.2 %all-to-all-done.1 = bf16[4,512,1024]{2,1,0:T(8,128)(2,1)} async-done(((bf16[4,512,1024]{2,1,0:T(8,128)(2,1)}), bf16[4,512,1024]{2,1,0:T(8,128)(2,1)}, u32[]{:S(2)}, u32[]{:S(2)}) %all-to-all-start.1) | async-done | bytes 4194336 | tf_op jit(solution)/shard_map/all_to_all | solution.py:186
  261.2 40.6 %shard_map.237 = bf16[2048,1024]{1,0:T(8,128)(2,1)S(1)} custom-call(f32[3,256,128]{2,1,0:T(8,128)S(1)} %pad_maximum_fusion.4.tabs_ref, bf16[2048,3072]{1,0:T(8,128)(2,1)} %add_convert_fusion.3.qkv_ref), custom_call_target="tpu_custom_call" | custom-call | flops 8589934592 | bytes 16777216 | tf_op jit(solution)/shard_map/pallas_call | solution.py:141
  314.8 29.8 %multiply_convert_fusion.3 = (bf16[2048,4096]{1,0:T(8,128)(2,1)}, f32[2048,4096]{1,0:T(8,128)}) fusion(f32[4096]{0:T(1024)S(1)} %bitcast.232, bf16[2048,1024]{1,0:T(8,128)(2,1)} %get-tuple-element.70, bf16[4096,1024]{1,0:T(8,128)(2,1)} %all-gather.18.cloned.1.call-done), kind=kOutput, calls=%fused_computation.30 | convolution fusion | flops 17230200832 | bytes 62930944 | tf_op jit(solution)/shard_map/dot_general | solution.py:22
  405.0 40.6 %shard_map.238 = bf16[2048,1024]{1,0:T(8,128)(2,1)S(1)} custom-call(f32[3,256,128]{2,1,0:T(8,128)S(1)} %pad_maximum_fusion.4.tabs_ref, bf16[2048,3072]{1,0:T(8,128)(2,1)} %add_convert_fusion.2.qkv_ref), custom_call_target="tpu_custom_call" | custom-call | flops 8589934592 | bytes 16777216 | tf_op jit(solution)/shard_map/pallas_call | solution.py:141
  456.3 31.4 %multiply_convert_fusion.2 = (bf16[2048,4096]{1,0:T(8,128)(2,1)}, f32[2048,4096]{1,0:T(8,128)}) fusion(f32[4096]{0:T(1024)S(1)} %bitcast.234, bf16[4096,1024]{1,0:T(8,128)(2,1)} %all-gather.22.cloned.1.call-done, bf16[2048,1024]{1,0:T(8,128)(2,1)} %copy-done.13, f32[1024]{0:T(1024)S(1)} %bitcast.252, f32[1024]{0:T(1024)S(1)} %bitcast.244, ...), kind=kOutput, calls=%fused_computation.28 | convolution fusion | flops 17242783744 | bytes 62955520 | tf_op jit(solution)/shard_map/dot_general | solution.py:22
  533.5 40.6 %shard_map.239 = bf16[2048,1024]{1,0:T(8,128)(2,1)S(1)} custom-call(f32[3,256,128]{2,1,0:T(8,128)S(1)} %pad_maximum_fusion.4.tabs_ref, bf16[2048,3072]{1,0:T(8,128)(2,1)} %add_convert_fusion.1.qkv_ref), custom_call_target="tpu_custom_call" | custom-call | flops 8589934592 | bytes 16777216 | tf_op jit(solution)/shard_map/pallas_call | solution.py:141
  584.5 31.3 %multiply_convert_fusion.1 = (bf16[2048,4096]{1,0:T(8,128)(2,1)}, f32[2048,4096]{1,0:T(8,128)}) fusion(f32[4096]{0:T(1024)S(1)} %bitcast.236, bf16[4096,1024]{1,0:T(8,128)(2,1)} %all-gather.26.cloned.1.call-done, bf16[2048,1024]{1,0:T(8,128)(2,1)} %copy-done.17, f32[1024]{0:T(1024)S(1)} %bitcast.262, f32[1024]{0:T(1024)S(1)} %bitcast.254, ...), kind=kOutput, calls=%fused_computation.26 | convolution fusion | flops 17242783744 | bytes 62955520 | tf_op jit(solution)/shard_map/dot_general | solution.py:22
  615.8 26.3 %convert_reduce_fusion.4 = (f32[2048]{0:T(1024)S(1)}, bf16[2048,1024]{1,0:T(8,128)(2,1)S(1)}) fusion(f32[1024]{0:T(1024)S(1)} %bitcast.277, bf16[2048,4096]{1,0:T(8,128)(2,1)} %get-tuple-element.286, bf16[4096,1024]{1,0:T(8,128)(2,1)} %all-gather.28.cloned.1.call-done, f32[1024]{0:T(1024)S(1)} %bitcast.278, f32[2048,1024]{1,0:T(8,128)} %fusion.130, ...), kind=kOutput, calls=%fused_computation.43 | convolution fusion | flops 17196644352 | bytes 41959424 | tf_op jit(solution)/shard_map/dot_general | solution.py:22
  662.7 40.6 %shard_map.240 = bf16[2048,1024]{1,0:T(8,128)(2,1)S(1)} custom-call(f32[3,256,128]{2,1,0:T(8,128)S(1)} %pad_maximum_fusion.4.tabs_ref, bf16[2048,3072]{1,0:T(8,128)(2,1)} %add_convert_fusion.qkv_ref), custom_call_target="tpu_custom_call" | custom-call | flops 8589934592 | bytes 16777216 | tf_op jit(solution)/shard_map/pallas_call | solution.py:141
  713.8 30.5 %multiply_convert_fusion = (bf16[2048,4096]{1,0:T(8,128)(2,1)}, f32[2048,4096]{1,0:T(8,128)}) fusion(f32[4096]{0:T(1024)S(1)} %bitcast.238, bf16[4096,1024]{1,0:T(8,128)(2,1)} %all-gather.30.cloned.1.call-done, bf16[2048,1024]{1,0:T(8,128)(2,1)} %copy-done.7, f32[1024]{0:T(1024)S(1)} %bitcast.273, f32[1024]{0:T(1024)S(1)} %bitcast.264, ...), kind=kOutput, calls=%fused_computation.24 | convolution fusion | flops 17242783744 | bytes 62955520 | tf_op jit(solution)/shard_map/dot_general | solution.py:22
  744.3 25.5 %fusion.105 = bf16[2048,1024]{1,0:T(8,128)(2,1)} fusion(f32[2048,1024]{1,0:T(8,128)} %fusion.127, bf16[2048,1024]{1,0:T(8,128)(2,1)} %copy-done.7, bf16[2048,4096]{1,0:T(8,128)(2,1)} %get-tuple-element.290, bf16[4096,1024]{1,0:T(8,128)(2,1)} %all-gather.32.cloned.1.call-done, f32[1024]{0:T(1024)S(1)} %bitcast.276, f32[1024]{0:T(1024)S(1)} %bitcast.275), kind=kOutput, calls=%fused_computation.144 | convolution fusion | flops 17192452096 | bytes 41951232 | tf_op jit(solution)/shard_map/dot_general | solution.py:22
  800.9 38.6 %fusion.173 = (f32[4096]{0:T(1024)}, bf16[2048,4096]{1,0:T(8,128)(2,1)}) fusion(f32[2048,4096]{1,0:T(8,128)} %get-tuple-element.291, f32[4096]{0:T(1024)S(1)} %bitcast.239, bf16[2048,1024]{1,0:T(8,128)(2,1)} %bitcast.199, bf16[4096,1024]{1,0:T(8,128)(2,1)} %all-gather.32.cloned.1.call-done), kind=kOutput, calls=%fused_computation.290 | convolution fusion | flops 17280528384 | bytes 62947328 | tf_op jit(solution)/shard_map/dot_general | solution.py:22
  882.1 80.2 %shard_map.241 = bf16[2048,3072]{1,0:T(8,128)(2,1)} custom-call(f32[3,256,128]{2,1,0:T(8,128)S(1)} %pad_maximum_fusion.4.tabs_ref, bf16[2048,3072]{1,0:T(8,128)(2,1)} %add_convert_fusion.qkv_ref, bf16[2048,1024]{1,0:T(8,128)(2,1)S(1)} %convolution_convert_fusion.15.gctx_ref), custom_call_target="tpu_custom_call" | custom-call | flops 21474836480 | bytes 29360128 | tf_op jit(solution)/shard_map/pallas_call | solution.py:141
  999.9 30.6 %fusion.162 = (f32[1024]{0:T(1024)}, f32[1024]{0:T(1024)}, f32[2048]{0:T(1024)S(1)}, f32[2048]{0:T(1024)S(1)}, f32[2048,1024]{1,0:T(8,128)}, /*index=5*/f32[1024]{0:T(1024)}, f32[1024]{0:T(1024)}) fusion(f32[2048]{0:T(1024)S(1)} %copy-done.53, f32[2048]{0:T(1024)S(1)} %copy-done.45, bf16[2048,1024]{1,0:T(8,128)(2,1)S(1)} %copy-done.10, ...), kind=kOutput, calls=%fused_computation.282 | convolution fusion | flops 17211322368 | bytes 46194688 | tf_op jit(solution)/shard_map/dot_general | solution.py:22
  1064.6 39.5 %fusion.172 = (f32[4096]{0:T(1024)}, bf16[2048,4096]{1,0:T(8,128)(2,1)}) fusion(f32[2048,4096]{1,0:T(8,128)} %get-tuple-element.287, f32[4096]{0:T(1024)S(1)} %bitcast.237, bf16[2048,1024]{1,0:T(8,128)(2,1)} %copy-done.12, bf16[4096,1024]{1,0:T(8,128)(2,1)} %all-gather.28.cloned.1.call-done), kind=kOutput, calls=%fused_computation.289 | convolution fusion | flops 17280528384 | bytes 62947328 | tf_op jit(solution)/shard_map/dot_general | solution.py:22
  1147.6 80.4 %shard_map.242 = bf16[2048,3072]{1,0:T(8,128)(2,1)} custom-call(f32[3,256,128]{2,1,0:T(8,128)S(1)} %pad_maximum_fusion.4.tabs_ref, bf16[2048,3072]{1,0:T(8,128)(2,1)} %add_convert_fusion.1.qkv_ref, bf16[2048,1024]{1,0:T(8,128)(2,1)S(1)} %convolution_convert_fusion.14.gctx_ref), custom_call_target="tpu_custom_call" | custom-call | flops 21474836480 | bytes 29360128 | tf_op jit(solution)/shard_map/pallas_call | solution.py:141
  1265.7 28.0 %fusion.160 = (f32[1024]{0:T(1024)}, f32[1024]{0:T(1024)}, f32[2048]{0:T(1024)S(1)}, f32[2048]{0:T(1024)S(1)}, f32[2048,1024]{1,0:T(8,128)}, /*index=5*/f32[1024]{0:T(1024)}, f32[1024]{0:T(1024)}) fusion(f32[2048]{0:T(1024)S(1)} %copy-done.51, f32[2048]{0:T(1024)S(1)} %copy-done.43, bf16[2048,1024]{1,0:T(8,128)(2,1)S(1)} %copy-done.20, ...), kind=kOutput, calls=%fused_computation.280 | convolution fusion | flops 17211322368 | bytes 46194688 | tf_op jit(solution)/shard_map/dot_general | solution.py:22
  1328.3 38.1 %fusion.171 = (f32[4096]{0:T(1024)}, bf16[2048,4096]{1,0:T(8,128)(2,1)}) fusion(f32[2048,4096]{1,0:T(8,128)} %get-tuple-element.283, f32[4096]{0:T(1024)S(1)} %bitcast.235, bf16[2048,1024]{1,0:T(8,128)(2,1)} %copy-done.21, bf16[4096,1024]{1,0:T(8,128)(2,1)} %all-gather.24.cloned.1.call-done), kind=kOutput, calls=%fused_computation.288 | convolution fusion | flops 17280528384 | bytes 62947328 | tf_op jit(solution)/shard_map/dot_general | solution.py:22
  1406.3 80.2 %shard_map.243 = bf16[2048,3072]{1,0:T(8,128)(2,1)} custom-call(f32[3,256,128]{2,1,0:T(8,128)S(1)} %pad_maximum_fusion.4.tabs_ref, bf16[2048,3072]{1,0:T(8,128)(2,1)} %add_convert_fusion.2.qkv_ref, bf16[2048,1024]{1,0:T(8,128)(2,1)S(1)} %convolution_convert_fusion.13.gctx_ref), custom_call_target="tpu_custom_call" | custom-call | flops 21474836480 | bytes 29360128 | tf_op jit(solution)/shard_map/pallas_call | solution.py:141
  1525.1 31.9 %fusion.158 = (f32[1024]{0:T(1024)}, f32[1024]{0:T(1024)}, f32[2048]{0:T(1024)S(1)}, f32[2048]{0:T(1024)S(1)}, f32[2048,1024]{1,0:T(8,128)S(1)}, /*index=5*/f32[1024]{0:T(1024)}, f32[1024]{0:T(1024)}) fusion(f32[2048]{0:T(1024)S(1)} %copy-done.49, f32[2048]{0:T(1024)S(1)} %copy-done.41, bf16[2048,1024]{1,0:T(8,128)(2,1)} %copy-done.13, ...), kind=kOutput, calls=%fused_computation.278 | convolution fusion | flops 17211322368 | bytes 46194688 | tf_op jit(solution)/shard_map/dot_general | solution.py:22
  1587.0 38.6 %fusion.170 = (f32[4096]{0:T(1024)}, bf16[2048,4096]{1,0:T(8,128)(2,1)S(1)}) fusion(f32[2048,4096]{1,0:T(8,128)} %get-tuple-element.279, f32[4096]{0:T(1024)S(1)} %bitcast.233, bf16[2048,1024]{1,0:T(8,128)(2,1)} %copy-done.26, bf16[4096,1024]{1,0:T(8,128)(2,1)} %all-gather.20.cloned.1.call-done), kind=kOutput, calls=%fused_computation.287 | convolution fusion | flops 17280528384 | bytes 62947328 | tf_op jit(solution)/shard_map/dot_general | solution.py:22
  1665.7 80.2 %shard_map.244 = bf16[2048,3072]{1,0:T(8,128)(2,1)} custom-call(f32[3,256,128]{2,1,0:T(8,128)S(1)} %pad_maximum_fusion.4.tabs_ref, bf16[2048,3072]{1,0:T(8,128)(2,1)} %add_convert_fusion.3.qkv_ref, bf16[2048,1024]{1,0:T(8,128)(2,1)S(1)} %convolution_convert_fusion.12.gctx_ref), custom_call_target="tpu_custom_call" | custom-call | flops 21474836480 | bytes 29360128 | tf_op jit(solution)/shard_map/pallas_call | solution.py:141
  1865.5 56.1 %all-to-all-done.5 = bf16[4,512,1024]{2,1,0:T(8,128)(2,1)} async-done(((bf16[4,512,1024]{2,1,0:T(8,128)(2,1)}), bf16[4,512,1024]{2,1,0:T(8,128)(2,1)}, u32[]{:S(2)}, u32[]{:S(2)}) %all-to-all-start.5) | async-done | bytes 4194336 | tf_op jit(solution)/shard_map/all_to_all | solution.py:186
  (486 shorter events, 880.4 us)
Async XLA Ops:
  7.2 219.4 %all-gather.14.cloned.1.call-start = ((), (), s32[]{:S(2)}) async-start(), calls=%async_computation.19 | async-start | bytes 28311552 | tf_op jit(solution)/shard_map/all_gather | solution.py:191
  11.3 292.7 %all-gather.16.cloned.1.call-start = ((), (), s32[]{:S(2)}) async-start(), calls=%async_computation.20 | async-start | bytes 9437184 | tf_op jit(solution)/shard_map/all_gather | solution.py:191
  145.0 169.8 %all-gather.18.cloned.1.call-start = ((), (), s32[]{:S(2)}) async-start(), calls=%async_computation.21 | async-start | bytes 9437184 | tf_op jit(solution)/shard_map/all_gather | solution.py:183
  230.8 128.6 %all-gather.20.cloned.1.call-start = ((), (), s32[]{:S(2)}) async-start(), calls=%async_computation.22 | async-start | bytes 9437184 | tf_op jit(solution)/shard_map/all_gather | solution.py:183
  236.2 220.0 %all-gather.22.cloned.1.call-start = ((), (), s32[]{:S(2)}) async-start(), calls=%async_computation.23 | async-start | bytes 9437184 | tf_op jit(solution)/shard_map/all_gather | solution.py:183
  236.8 250.8 %all-gather.24.cloned.1.call-start = ((), (), s32[]{:S(2)}) async-start(), calls=%async_computation.24 | async-start | bytes 9437184 | tf_op jit(solution)/shard_map/all_gather | solution.py:183
  237.4 347.0 %all-gather.26.cloned.1.call-start = ((), (), s32[]{:S(2)}) async-start(), calls=%async_computation.25 | async-start | bytes 9437184 | tf_op jit(solution)/shard_map/all_gather | solution.py:183
  238.1 377.6 %all-gather.28.cloned.1.call-start = ((), (), s32[]{:S(2)}) async-start(), calls=%async_computation.26 | async-start | bytes 9437184 | tf_op jit(solution)/shard_map/all_gather | solution.py:183
  238.9 474.8 %all-gather.30.cloned.1.call-start = ((), (), s32[]{:S(2)}) async-start(), calls=%async_computation.27 | async-start | bytes 9437184 | tf_op jit(solution)/shard_map/all_gather | solution.py:183
  239.6 504.6 %all-gather.32.cloned.1.call-start = ((), (), s32[]{:S(2)}) async-start(), calls=%async_computation.28 | async-start | bytes 9437184 | tf_op jit(solution)/shard_map/all_gather | solution.py:183
  303.9 677.8 %all-gather.34.cloned.1.call-start = ((), (), s32[]{:S(2)}) async-start(), calls=%async_computation.29 | async-start | bytes 37748736 | tf_op jit(solution)/shard_map/all_gather | solution.py:183
  769.8 477.7 %reduce-scatter.16.cloned.1.call-start = ((), (), s32[]{:S(2)}) async-start(), calls=%async_computation.31 | async-start | bytes 9437184 | tf_op jit(solution)/shard_map/reduce_scatter | solution.py:250
  864.6 382.9 %reduce-scatter.14.cloned.1.call-start = ((), (), s32[]{:S(2)}) async-start(), calls=%async_computation.30 | async-start | bytes 9437184 | tf_op jit(solution)/shard_map/reduce_scatter | solution.py:250
  874.2 373.3 %reduce-scatter.18.cloned.1.call-start = ((), (), s32[]{:S(2)}) async-start(), calls=%async_computation.32 | async-start | bytes 7077888 | tf_op jit(solution)/shard_map/reduce_scatter | solution.py:250
  1030.6 475.2 %reduce-scatter.22.cloned.1.call-start = ((), (), s32[]{:S(2)}) async-start(), calls=%async_computation.34 | async-start | bytes 9437184 | tf_op jit(solution)/shard_map/reduce_scatter | solution.py:250
  1128.9 376.8 %reduce-scatter.20.cloned.1.call-start = ((), (), s32[]{:S(2)}) async-start(), calls=%async_computation.33 | async-start | bytes 9437184 | tf_op jit(solution)/shard_map/reduce_scatter | solution.py:250
  1139.4 366.4 %reduce-scatter.24.cloned.1.call-start = ((), (), s32[]{:S(2)}) async-start(), calls=%async_computation.35 | async-start | bytes 7077888 | tf_op jit(solution)/shard_map/reduce_scatter | solution.py:250
  1293.8 469.5 %reduce-scatter.28.cloned.1.call-start = ((), (), s32[]{:S(2)}) async-start(), calls=%async_computation.37 | async-start | bytes 9437184 | tf_op jit(solution)/shard_map/reduce_scatter | solution.py:250
  1391.5 371.8 %reduce-scatter.26.cloned.1.call-start = ((), (), s32[]{:S(2)}) async-start(), calls=%async_computation.36 | async-start | bytes 9437184 | tf_op jit(solution)/shard_map/reduce_scatter | solution.py:250
  1392.3 371.0 %reduce-scatter.30.cloned.1.call-start = ((), (), s32[]{:S(2)}) async-start(), calls=%async_computation.38 | async-start | bytes 7077888 | tf_op jit(solution)/shard_map/reduce_scatter | solution.py:250
  1525.0 324.6 %reduce-scatter.38.cloned.1.call-start = ((), (), s32[]{:S(2)}) async-start(), calls=%async_computation.42 | async-start | bytes 9437184 | tf_op jit(solution)/shard_map/reduce_scatter | solution.py:250
  1586.3 276.0 %reduce-scatter.36.cloned.1.call-start = ((), (), s32[]{:S(2)}) async-start(), calls=%async_computation.41 | async-start | bytes 9437184 | tf_op jit(solution)/shard_map/reduce_scatter | solution.py:250
  1651.5 298.0 %reduce-scatter.32.cloned.1.call-start = ((), (), s32[]{:S(2)}) async-start(), calls=%async_computation.39 | async-start | bytes 7077888 | tf_op jit(solution)/shard_map/reduce_scatter | solution.py:250
  1763.4 255.9 %reduce-scatter.34.cloned.1.call-start = ((), (), s32[]{:S(2)}) async-start(), calls=%async_computation.40 | async-start | bytes 9437184 | tf_op jit(solution)/shard_map/reduce_scatter | solution.py:288
  (130 other events, 3516.4 us)
Sparse Core Ops, SparseCore 0:
  11.4 186.8 all-gather.13
  200.1 57.6 all-gather.15
  260.2 48.6 all-gather.17
  310.6 48.6 all-gather.19
  361.0 48.6 all-gather.21
  411.5 48.8 all-gather.23
  462.7 48.6 all-gather.25
  513.8 48.6 all-gather.27
  565.0 48.7 all-gather.29
  615.4 48.6 all-gather.31
  769.9 154.0 all-gather.33
  927.8 63.1 reduce-scatter.15
  994.4 63.1 reduce-scatter.13
  1061.3 53.4 reduce-scatter.17
  1129.1 61.8 reduce-scatter.21
  1194.2 63.1 reduce-scatter.19
  1293.9 52.0 reduce-scatter.23
  1391.6 61.8 reduce-scatter.27
  1456.9 63.1 reduce-scatter.25
  1525.1 52.1 reduce-scatter.29
  1586.4 61.7 reduce-scatter.37
  1651.6 63.1 reduce-scatter.35
  1763.5 52.0 reduce-scatter.31
  1818.8 85.9 reduce-scatter.33
